TPU v7x, 512 devices: a whole 4x8x8 slice. The times are simulated.
512 devices in a mesh: dp: 32 (over z, x), mp: 16 (over y, core).
Axes of the slice: x: 4, y: 8, z: 8, core: 2. Of those that a mesh axis runs over, the one named last changes fastest.
Arguments:
- hidden_acts: bfloat16 [32768, 8192], P('dp', 'mp'), may hold values from -12 to 12
- out_cotangent: bfloat16 [32768, 1024], P('dp'), may hold values from -0.003314563 to 0.003314563
- left_stats: float32 [128, 512, 512], P('dp', 'mp'), may hold values from -0.35355339 to 5.3535534
- right_stats: float32 [128, 512, 512], P('dp', 'mp'), may hold values from -0.35355339 to 5.3535534
- left_roots: bfloat16 [128, 512, 512], P('dp', 'mp'), may hold values from -0.088388348 to 1.0883883
- right_roots: bfloat16 [128, 512, 512], P('dp', 'mp'), may hold values from -0.088388348 to 1.0883883
- owner_map: int32 [32], replicated, may hold values from 0 to 31, as said below
- owner_counts: int32 [32], replicated, may hold values from 0 to 4, as said below
Outputs:
- update: bfloat16 [32, 512, 512], P('dp', 'mp')
- new_left: float32 [128, 512, 512], P('dp', 'mp')
- new_right: float32 [128, 512, 512], P('dp', 'mp')
Inputs may be any that keep to these rules, and one draw needn't show every extreme that they name: owner_map[b] is the dp index that keeps block b's statistics; index d owns exactly owner_counts[d] blocks, at most 4, and some index owns exactly 4 in every draw. owner_counts[d] is the number of blocks b with owner_map[b] = d; the counts sum to 32.
All inputs are finite; a program needn't handle non-finite values.
Results may differ from a plain program's by a relative error of at most 0.018.
Values may be sent and summed in bfloat16 or wider, within the bound.
A program may use at most 64 MiB of HBM per device.

v0:
```python
import jax
import jax.numpy as jnp
from jax import lax
from jax.sharding import PartitionSpec as P

epsilon = 1e-06


def split_up(value, dim, length):
    lengths = value.shape
    pieces = value.reshape(*lengths[:dim], length, lengths[dim] // length, *lengths[dim + 1 :])
    return jnp.moveaxis(pieces, dim, 0)


def sum_at_owner(value, axis, dim):
    length = lax.axis_size(axis)
    pieces = lax.all_to_all(split_up(value, dim, length), axis, 0, 0, tiled=True)
    return jnp.sum(pieces.astype(jnp.float32), axis=0)


def side_by_side(arrays, axis, dim, along):
    ends, at = ([], 0)
    for a in arrays[:-1]:
        at += a.shape[along]
        ends.append(at)
    both = jnp.concatenate(arrays, axis=along)
    return tuple(jnp.split(lax.all_gather(both, axis, axis=dim, tiled=True), ends, axis=along))


def from_everyone(value, axis):
    copies = jnp.broadcast_to(value, (lax.axis_size(axis), *value.shape))
    return lax.all_to_all(copies, axis, split_axis=0, concat_axis=0, tiled=True)


def over_copies(value, axis):
    everything = from_everyone(value, axis)
    return jnp.sum(everything, axis=0)


def precondition(full_grad, full_root, own_rows, left_root, column, rows_piece):
    left_add = jnp.einsum("srk,stk->srt", own_rows, full_grad, preferred_element_type=jnp.float32)
    own_cols = lax.dynamic_slice_in_dim(full_grad, column * rows_piece, rows_piece, 2)
    right_add = jnp.einsum("skr,skt->srt", own_cols, full_grad, preferred_element_type=jnp.float32)
    applied = jnp.einsum(
        "srk,skt->srt", left_root, full_grad, preferred_element_type=jnp.float32
    ).astype(jnp.bfloat16)
    conditioned = jnp.einsum("srk,skt->srt", applied, full_root, preferred_element_type=jnp.float32)
    widened = full_grad.astype(jnp.float32)
    grad_square = jnp.sum(widened * widened, axis=(1, 2))
    return (left_add, right_add, conditioned, grad_square)


def graft_update(conditioned, grad_square, cond_square, block_width):
    entries = float(block_width * block_width)
    scale_ratio = jnp.sqrt((grad_square / entries + epsilon) / (cond_square / entries + epsilon))
    return (conditioned * scale_ratio[:, None, None]).astype(jnp.bfloat16)


def shards(
    hidden_acts,
    out_cotangent,
    left_stats,
    right_stats,
    left_roots,
    right_roots,
    owner_map,
    owner_counts,
):
    devices = lax.axis_size("dp")
    myself = lax.axis_index("dp")
    column = lax.axis_index("mp")
    capacity, rows_piece, block_width = left_stats.shape
    blocks = owner_map.shape[0]
    per_home = blocks // devices
    partial_value = lax.dot_general(
        hidden_acts, out_cotangent, (((0,), (0,)), ((), ())), preferred_element_type=jnp.float32
    )
    band_rows = partial_value.shape[0] // rows_piece
    col_blocks = partial_value.shape[1] // block_width
    pieces = partial_value.reshape(band_rows, rows_piece, col_blocks, block_width).transpose(
        0, 2, 1, 3
    )
    pieces = pieces.reshape(blocks, rows_piece, block_width)
    block_ids = jnp.arange(blocks, dtype=jnp.int32)
    owners = jnp.arange(devices, dtype=jnp.int32)
    same_owner = owner_map[:, None] == owner_map[None, :]
    owner_rank = jnp.sum(
        (same_owner & (block_ids[None, :] < block_ids[:, None])).astype(jnp.int32), axis=1
    )
    held_count = jnp.sum(
        jnp.where(owner_map[:, None] == owners[None, :], owner_counts[None, :], 0), axis=1
    )
    is_live = (owner_rank < held_count) & (owner_rank < capacity)
    places = jnp.arange(capacity, dtype=jnp.int32)
    picked = (
        (owner_map[None, :] == myself) & (owner_rank[None, :] == places[:, None]) & is_live[None, :]
    )
    slot_block = jnp.sum(jnp.where(picked, block_ids[None, :], 0), axis=1)
    slot_live = jnp.any(picked, axis=1)
    home_ids = myself * per_home + jnp.arange(per_home, dtype=jnp.int32)
    home_owner = jnp.sum(
        jnp.where(block_ids[None, :] == home_ids[:, None], owner_map[None, :], 0), axis=1
    )
    home_rows = sum_at_owner(pieces.astype(jnp.bfloat16), "dp", 0).astype(jnp.bfloat16)
    to_owner_mask = home_owner[None, :] == owners[:, None]
    outgoing = jnp.where(
        to_owner_mask[:, :, None, None], home_rows[None], jnp.zeros((), jnp.bfloat16)
    )
    arrived = lax.all_to_all(outgoing, "dp", split_axis=0, concat_axis=0, tiled=True).reshape(
        blocks, rows_piece, block_width
    )
    grad_rows = jnp.where(
        slot_live[:, None, None], arrived[slot_block], jnp.zeros((), jnp.bfloat16)
    )
    full_grad, full_root = side_by_side((grad_rows, right_roots), "mp", 1, 0)
    left_add, right_add, conditioned, grad_square = precondition(
        full_grad, full_root, grad_rows, left_roots, column, rows_piece
    )
    cond_square = over_copies(jnp.sum(conditioned * conditioned, axis=(1, 2)), "mp")
    update_rows = graft_update(conditioned, grad_square, cond_square, block_width)
    new_left = left_stats + left_add
    new_right = right_stats + right_add
    owned_live = (owner_map == myself) & is_live
    safe_rank = jnp.minimum(owner_rank, capacity - 1)
    returning = jnp.where(
        owned_live[:, None, None], update_rows[safe_rank], jnp.zeros((), jnp.bfloat16)
    )
    returned = lax.all_to_all(
        returning.reshape(devices, per_home, rows_piece, block_width),
        "dp",
        split_axis=0,
        concat_axis=0,
        tiled=True,
    )
    from_owner = home_owner[None, :] == owners[:, None]
    update = jnp.sum(
        jnp.where(from_owner[:, :, None, None], returned, jnp.zeros((), jnp.bfloat16)),
        axis=0,
        dtype=jnp.float32,
    )
    return (update.astype(jnp.bfloat16), new_left, new_right)


def solution(mesh):
    in_specs = (
        P("dp", "mp"),
        P("dp", None),
        P("dp", "mp", None),
        P("dp", "mp", None),
        P("dp", "mp", None),
        P("dp", "mp", None),
        P(),
        P(),
    )
    out_specs = (P("dp", "mp", None), P("dp", "mp", None), P("dp", "mp", None))
    return jax.shard_map(shards, mesh=mesh, in_specs=in_specs, out_specs=out_specs, check_vma=False)
```

profile of v0, /device:TPU:1, one launch (start us, length us, event | category | flops | bytes accessed | tf_op | source)
XLA Modules:
  0.0 195.6 jit_solution(8219461290951562862)
XLA Ops:
  7.2 1.6 copy-done
  8.8 3.5 %convolution_convert_fusion = bf16[512,1024]{1,0:T(8,128)(2,1)} fusion(bf16[1024,512]{1,0:T(8,128)(2,1)} %param.8, bf16[1024,1024]{1,0:T(8,128)(2,1)S(1)} %copy-done), kind=kOutput, calls=%fused_computation.5 | convolution fusion | flops 1074266112 | bytes 4194304 | tf_op jit(solution)/shard_map/dot_general | solution.py:75
  12.2 1.8 convert_element_type.38
  14.1 1.2 copy.26
  15.3 13.7 %all-to-all-start = ((bf16[32,1,32,512]{3,2,1,0:T(8,128)(2,1)}), bf16[32,1,32,512]{3,2,1,0:T(8,128)(2,1)S(1)}, u32[]{:S(2)}, u32[]{:S(2)}) async-start(bf16[32,1,32,512]{3,2,1,0:T(8,128)(2,1)} %bitcast.32), calls=%async_computation | async-start | bytes 2097152 | tf_op jit(solution)/shard_map/all_to_all | solution.py:17
  29.0 0.6 fusion.8
  29.7 0.6 iota_compare_fusion.3
  30.3 24.9 %all-to-all-done = bf16[32,1,32,512]{3,2,1,0:T(8,128)(2,1)S(1)} async-done(((bf16[32,1,32,512]{3,2,1,0:T(8,128)(2,1)}), bf16[32,1,32,512]{3,2,1,0:T(8,128)(2,1)S(1)}, u32[]{:S(2)}, u32[]{:S(2)}) %all-to-all-start) | async-done | bytes 1048608 | tf_op jit(solution)/shard_map/all_to_all | solution.py:17
  55.4 1.1 select_bitcast_fusion
  56.5 6.4 %all-to-all-start.1 = ((bf16[32,1,32,512]{3,2,1,0:T(8,128)(2,1)}), bf16[32,1,32,512]{3,2,1,0:T(8,128)(2,1)S(1)}, u32[]{:S(2)}, u32[]{:S(2)}) async-start(bf16[32,1,32,512]{3,2,1,0:T(8,128)(2,1)} %select_bitcast_fusion), calls=%async_computation.1 | async-start | bytes 2097152 | tf_op jit(solution)/shard_map/all_to_all | solution.py:109
  63.4 24.9 %all-to-all-done.1 = bf16[32,1,32,512]{3,2,1,0:T(8,128)(2,1)S(1)} async-done(((bf16[32,1,32,512]{3,2,1,0:T(8,128)(2,1)}), bf16[32,1,32,512]{3,2,1,0:T(8,128)(2,1)S(1)}, u32[]{:S(2)}, u32[]{:S(2)}) %all-to-all-start.1) | async-done | bytes 1048608 | tf_op jit(solution)/shard_map/all_to_all | solution.py:109
  88.9 0.7 pad_maximum_fusion
  89.7 45.0 %all-gather.2.cloned.1.call-done = bf16[8,512,512]{2,1,0:T(8,128)(2,1)} async-done(((bf16[8,32,512]{2,1,0:T(8,128)(2,1)}), bf16[8,512,512]{2,1,0:T(8,128)(2,1)}) %all-gather.2.cloned.1.call-update) | async-done | bytes 4194320 | tf_op jit(solution)/shard_map/all_gather | solution.py:27
  134.7 3.2 %multiply_reduce_fusion.1 = (f32[4]{0:T(128)S(1)}, f32[4,32,512]{2,1,0:T(8,128)S(1)}) fusion(bf16[8,512,512]{2,1,0:T(8,128)(2,1)} %all-gather.2.cloned.1.call-done, bf16[4,32,512]{2,1,0:T(8,128)(2,1)} %param.12), kind=kOutput, calls=%fused_computation.17 | convolution fusion | flops 134414336 | bytes 4587536 | tf_op jit(solution)/shard_map/srk,skt->srt/dot_general | solution.py:47
  138.5 4.5 %all-to-all-start.2 = ((f32[16,1,4]{2,1,0:T(1,128)}), f32[16,1,4]{2,1,0:T(1,128)S(1)}, u32[]{:S(2)}, u32[]{:S(2)}) async-start(f32[16,1,4]{2,1,0:T(1,128)} %broadcast_in_dim.118), calls=%async_computation.2 | async-start | bytes 16384 | tf_op jit(solution)/shard_map/all_to_all | solution.py:32
  142.9 2.2 %multiply_reduce_fusion = f32[4]{0:T(128)S(1)} fusion(bf16[8,512,512]{2,1,0:T(8,128)(2,1)} %all-gather.2.cloned.1.call-done), kind=kLoop, calls=%fused_computation.2 | loop fusion | flops 3145724 | bytes 2097168 | tf_op jit(solution)/shard_map/reduce_sum | solution.py:49
  145.1 4.7 %all-to-all-done.2 = f32[16,1,4]{2,1,0:T(1,128)S(1)} async-done(((f32[16,1,4]{2,1,0:T(1,128)}), f32[16,1,4]{2,1,0:T(1,128)S(1)}, u32[]{:S(2)}, u32[]{:S(2)}) %all-to-all-start.2) | async-done | bytes 288 | tf_op jit(solution)/shard_map/all_to_all | solution.py:32
  150.7 1.1 fusion.3
  151.8 9.9 %all-to-all-start.3 = ((bf16[32,1,32,512]{3,2,1,0:T(8,128)(2,1)}), bf16[32,1,32,512]{3,2,1,0:T(8,128)(2,1)S(1)}, u32[]{:S(2)}, u32[]{:S(2)}) async-start(bf16[32,1,32,512]{3,2,1,0:T(8,128)(2,1)} %fusion.3), calls=%async_computation.3 | async-start | bytes 2097152 | tf_op jit(solution)/shard_map/all_to_all | solution.py:128
  161.7 1.6 slice-done
  163.3 2.6 %convolution_add_fusion = f32[4,32,512]{2,1,0:T(8,128)} fusion(f32[4,32,512]{2,1,0:T(8,128)} %param.11, bf16[4,512,512]{2,1,0:T(8,128)(2,1)S(1)} %slice-done, s32[]{:T(128)S(6)} %select_n.76), kind=kOutput, calls=%fused_computation.6 | convolution fusion | flops 67174400 | bytes 3145732 | tf_op jit(solution)/shard_map/skr,skt->srt/dot_general | solution.py:43
  165.9 1.4 convolution_add_fusion.1
  167.3 20.6 %all-to-all-done.3 = bf16[32,1,32,512]{3,2,1,0:T(8,128)(2,1)S(1)} async-done(((bf16[32,1,32,512]{3,2,1,0:T(8,128)(2,1)}), bf16[32,1,32,512]{3,2,1,0:T(8,128)(2,1)S(1)}, u32[]{:S(2)}, u32[]{:S(2)}) %all-to-all-start.3) | async-done | bytes 1048608 | tf_op jit(solution)/shard_map/all_to_all | solution.py:128
  187.9 0.8 fusion.2
  (30 shorter events, 2.7 us)
Async XLA Ops:
  7.2 1.6 copy-start
  14.1 14.9 %copy-start.4 = (s32[32]{0:T(128)S(1)}, s32[32]{0:T(128)}, u32[]{:S(2)}) copy-start(s32[32]{0:T(128)} %param.14) | copy-start | bytes 388
  15.3 39.9 %all-to-all-start = ((bf16[32,1,32,512]{3,2,1,0:T(8,128)(2,1)}), bf16[32,1,32,512]{3,2,1,0:T(8,128)(2,1)S(1)}, u32[]{:S(2)}, u32[]{:S(2)}) async-start(bf16[32,1,32,512]{3,2,1,0:T(8,128)(2,1)} %bitcast.32), calls=%async_computation | async-start | bytes 2097152 | tf_op jit(solution)/shard_map/all_to_all | solution.py:17
  30.3 32.6 %copy-start.5 = (s32[32]{0:T(128)S(1)}, s32[32]{0:T(128)}, u32[]{:S(2)}) copy-start(s32[32]{0:T(128)} %param.15) | copy-start | bytes 388
  55.4 33.5 %copy-start.3 = (bf16[4,32,512]{2,1,0:T(8,128)(2,1)S(1)}, bf16[4,32,512]{2,1,0:T(8,128)(2,1)}, u32[]{:S(2)}) copy-start(bf16[4,32,512]{2,1,0:T(8,128)(2,1)} %param.13) | copy-start | bytes 393220
  56.5 31.8 %all-to-all-start.1 = ((bf16[32,1,32,512]{3,2,1,0:T(8,128)(2,1)}), bf16[32,1,32,512]{3,2,1,0:T(8,128)(2,1)S(1)}, u32[]{:S(2)}, u32[]{:S(2)}) async-start(bf16[32,1,32,512]{3,2,1,0:T(8,128)(2,1)} %select_bitcast_fusion), calls=%async_computation.1 | async-start | bytes 2097152 | tf_op jit(solution)/shard_map/all_to_all | solution.py:109
  62.9 71.8 %all-gather.2.cloned.1.call-start = ((), (), s32[]{:S(2)}) async-start(), calls=%async_computation.4 | async-start | bytes 4456448 | tf_op jit(solution)/shard_map/all_gather | solution.py:27
  138.5 11.4 %all-to-all-start.2 = ((f32[16,1,4]{2,1,0:T(1,128)}), f32[16,1,4]{2,1,0:T(1,128)S(1)}, u32[]{:S(2)}, u32[]{:S(2)}) async-start(f32[16,1,4]{2,1,0:T(1,128)} %broadcast_in_dim.118), calls=%async_computation.2 | async-start | bytes 16384 | tf_op jit(solution)/shard_map/all_to_all | solution.py:32
  151.8 36.1 %all-to-all-start.3 = ((bf16[32,1,32,512]{3,2,1,0:T(8,128)(2,1)}), bf16[32,1,32,512]{3,2,1,0:T(8,128)(2,1)S(1)}, u32[]{:S(2)}, u32[]{:S(2)}) async-start(bf16[32,1,32,512]{3,2,1,0:T(8,128)(2,1)} %fusion.3), calls=%async_computation.3 | async-start | bytes 2097152 | tf_op jit(solution)/shard_map/all_to_all | solution.py:128
  161.7 1.6 slice-start
  161.7 4.2 %copy-start.1 = (bf16[8,512,512]{2,1,0:T(8,128)(2,1)S(1)}, bf16[8,512,512]{2,1,0:T(8,128)(2,1)}, u32[]{:S(2)}) copy-start(bf16[8,512,512]{2,1,0:T(8,128)(2,1)} %all-gather.2.cloned.1.call-done) | copy-start | bytes 12582916
  163.3 2.6 %copy-start.2 = (f32[4,32,512]{2,1,0:T(8,128)S(1)}, f32[4,32,512]{2,1,0:T(8,128)}, u32[]{:S(2)}) copy-start(f32[4,32,512]{2,1,0:T(8,128)} %param.10) | copy-start | bytes 786436
Sparse Core Ops, SparseCore 0:
  89.8 44.8 all-gather.1
where the time goes:
time: 198 us; the launch traced here: 196 us
  waiting for transfers between devices  120 us (61%)
  starting transfers between devices  34.5 us (17%)
  between operations  14.2 us (7%)
  matrix products  10.7 us (5%)
  other arithmetic  8.13 us (4%)
  local copies, waits for them, and re-layouts  8.02 us (4%)
    all_gather x1, waiting for transfers between devices, side_by_side(): lax.all_gather(both, axis, axis=dim, tiled=True)  45 us
    all_to_all x1, waiting for transfers between devices, sum_at_owner(): lax.all_to_all(split_up(value, dim, length), axis, 0, 0, tiled=True)  24.9 us
    all_to_all x1, waiting for transfers between devices, shards(): lax.all_to_all(outgoing, 'dp', split_axis=0, concat_axis=0, tiled=True)  24.9 us
    all_to_all x1, waiting for transfers between devices, shards(): lax.all_to_all(returning.reshape(devices, per_home, rows_piece, block_wid...  20.6 us
    all_to_all x1, starting transfers between devices, sum_at_owner(): lax.all_to_all(split_up(value, dim, length), axis, 0, 0, tiled=True)  13.7 us
    all_to_all x1, starting transfers between devices, shards(): lax.all_to_all(returning.reshape(devices, per_home, rows_piece, block_wid...  9.9 us
    all_to_all x1, starting transfers between devices, shards(): lax.all_to_all(outgoing, 'dp', split_axis=0, concat_axis=0, tiled=True)  6.37 us
    all_to_all x1, waiting for transfers between devices, from_everyone(): return lax.all_to_all(copies, axis, split_axis=0, concat_axis=0, tiled=True)  4.75 us
  transfers between devices with their start and end apart: 5, of which 5 were waited for; matrix products, arithmetic and copies ran while one was open for 4% of the time, Pallas kernels for 0%

commit v1 on v0

v1 whole, which is shorter than its diff:
```python
import functools

import jax
import jax.numpy as jnp
from jax import lax
from jax.experimental import pallas as pl
from jax.experimental.pallas import tpu as pltpu
from jax.sharding import PartitionSpec as P

epsilon = 1e-06
COLS = 4
MESH = pl.DeviceIdType.MESH
f32, bf16 = jnp.float32, jnp.bfloat16


def kernel(
    sizes,
    tab,
    acts,
    cot,
    lstat,
    rstat,
    lroot,
    rroot,
    upd,
    new_left,
    new_right,
    a_v,
    at_v,
    c_v,
    ls_v,
    rs_v,
    lr_v,
    rr_v,
    part,
    q,
    rel,
    xa,
    fwd,
    xsum,
    zr,
    gful,
    rful,
    rxs,
    rx,
    rzs,
    rz,
    slab,
    cond_v,
    ssq_s,
    ssq,
    zb,
    fxs,
    fx,
    loc,
    s_rx,
    r_rx,
    s_rz,
    r_rz,
    s_x1,
    r_x1,
    s_x2,
    r_x2,
    s_z,
    r_z,
    s_y,
    r_y,
    s_c,
    r_c,
    s_q,
    r_q,
    s_f,
    r_f,
    s_fx,
    r_fx,
):
    nz, ny, mp, rows, width, cap = sizes
    dp = lax.axis_index("dp")
    m = lax.axis_index("mp")
    x, z = dp % COLS, dp // COLS
    c, y = m % 2, m // 2
    half = nz // 2

    def at_x(k):
        return {"dp": z * COLS + (x + k) % COLS}

    def at_z(k):
        return {"dp": ((z + k) % nz) * COLS + x}

    def at_y(k):
        return {"mp": ((y + k) % ny) * 2 + c}

    def at_m(k):
        return {"mp": (m + k) % mp}

    partner = {"mp": y * 2 + (1 - c)}

    def send(src, dst, ssem, rsem, where):
        return pltpu.make_async_remote_copy(
            src_ref=src,
            dst_ref=dst,
            send_sem=ssem,
            recv_sem=rsem,
            device_id=where,
            device_id_type=MESH,
        )

    def loop(lo, hi, body):
        def step(i, carry):
            body(i)
            return carry

        lax.fori_loop(lo, hi, step, 0)

    loads = [
        pltpu.make_async_copy(s, d, loc.at[i])
        for i, (s, d) in enumerate(
            [(lroot, lr_v), (rroot, rr_v), (acts, a_v), (cot, c_v), (lstat, ls_v), (rstat, rs_v)]
        )
    ]
    for copy in loads:
        copy.start()

    barrier = pltpu.get_barrier_semaphore()

    def hello(where):
        pl.semaphore_signal(barrier, inc=1, device_id=where, device_id_type=MESH)

    for k in range(1, COLS):
        hello(at_x(k))
    loop(1, nz, lambda k: hello(at_z(k)))
    loop(1, mp, lambda k: hello(at_m(k)))

    loads[0].wait()
    loads[1].wait()
    start_me = tab[1, dp]

    def slot_for(col):
        return (col + 4 * COLS * nz - start_me) % COLS

    for k in range(1, COLS):
        r = slot_for((x + k) % COLS)
        rxs[k - 1, 0] = lr_v[r]
        rxs[k - 1, 1] = rr_v[r]
    r = slot_for(x)
    rx[x, 0] = lr_v[r]
    rx[x, 1] = rr_v[r]
    pl.semaphore_wait(barrier, COLS - 1 + nz - 1 + mp - 1)
    root_x = [
        send(rxs.at[k - 1], rx.at[x], s_rx.at[k - 1], r_rx.at[k - 1], at_x(k)) for k in range(1, COLS)
    ]
    for copy in root_x:
        copy.start()

    loads[2].wait()
    tiles = a_v.shape[1] // 128

    def turn(i):
        at_v[pl.ds(i * 128, 128), :] = a_v[:, pl.ds(pl.multiple_of(i * 128, 128), 128)].T

    loop(0, tiles, turn)
    loads[3].wait()
    wide = 256
    per = width // wide

    def multiply(n):
        got = jnp.dot(
            at_v[...],
            c_v[:, pl.ds(pl.multiple_of(n * wide, wide), wide)],
            preferred_element_type=f32,
        )
        got = got.astype(bf16).reshape(part.shape[0], rows, wide)
        part[:, n // per, :, pl.ds(pl.multiple_of((n % per) * wide, wide), wide)] = got

    loop(0, c_v.shape[1] // wide, multiply)
    ncol = c_v.shape[1] // width

    def arrange(s):
        b = tab[2, s]
        q[s % COLS, s // COLS] = part[b // ncol, b % ncol]

    loop(0, COLS * nz, arrange)

    lo, hi = pl.ds(0, half), pl.ds(half, half)
    far, right, left = (x + 2) % COLS, (x + 1) % COLS, (x + 3) % COLS
    relay = [
        send(q.at[far, lo], rel.at[0], s_x1.at[0], r_x1.at[0], at_x(1)),
        send(q.at[far, hi], rel.at[1], s_x1.at[1], r_x1.at[1], at_x(3)),
    ]
    direct = [
        send(q.at[right, hi], xa.at[0], s_x1.at[2], r_x1.at[2], at_x(1)),
        send(q.at[left, lo], xa.at[1], s_x1.at[3], r_x1.at[3], at_x(3)),
    ]
    onward = [
        send(fwd.at[0], xa.at[2], s_x2.at[0], r_x2.at[0], at_x(1)),
        send(fwd.at[1], xa.at[3], s_x2.at[1], r_x2.at[1], at_x(3)),
    ]
    for copy in relay + direct:
        copy.start()

    for copy in root_x:
        copy.wait_recv()

    def root_row(k):
        row = (z + k) % nz
        xo = tab[3, row * COLS + x] % COLS
        rzs[row] = rx[xo]

    def root_send(k):
        return send(rzs.at[(z + k) % nz], rz.at[z], s_rz.at[k - 1], r_rz.at[k - 1], at_z(k))

    loop(0, nz, root_row)
    rz[z] = rzs[z]
    loop(1, nz, lambda k: root_send(k).start())

    for side, (toward, part_of) in enumerate([(right, lo), (left, hi)]):
        relay[side].wait_recv()
        fwd[side] = (q[toward, part_of].astype(f32) + rel[side].astype(f32)).astype(bf16)
        onward[side].start()
    for copy in direct + onward:
        copy.wait_recv()
    own = q[x].astype(f32)
    xsum[lo] = (own[:half] + xa[1].astype(f32) + xa[2].astype(f32)).astype(bf16)
    xsum[hi] = (own[half:] + xa[0].astype(f32) + xa[3].astype(f32)).astype(bf16)

    def z_send(k):
        return send(xsum.at[(z + k) % nz], zr.at[k - 1], s_z.at[k - 1], r_z.at[k - 1], at_z(k))

    loop(1, nz, lambda k: z_send(k).start())

    loop(1, nz, lambda k: root_send(k).wait_recv())
    source = tab[3, dp] // COLS
    rful[m] = rz[source, 1]

    def gather(full, which):
        def out(k):
            return send(full.at[m], full.at[m], s_y.at[which, k], r_y.at[which, k], at_y(k))

        def across(k):
            at = ((y + ny - k) % ny) * 2 + c
            return send(full.at[at], full.at[at], s_c.at[which, k], r_c.at[which, k], partner)

        return out, across

    r_out, r_across = gather(rful, 0)
    g_out, g_across = gather(gful, 1)
    loop(1, ny, lambda k: r_out(k).start())
    r_across(0).start()

    loop(1, nz, lambda k: z_send(k).wait_recv())
    total = xsum[z].astype(f32)
    for k in range(nz - 1):
        total = total + zr[k].astype(f32)
    gful[m] = total.astype(bf16)
    loop(1, ny, lambda k: g_out(k).start())
    g_across(0).start()

    def pass_on(out, across):
        def step(k):
            out(k).wait_recv()
            across(k).start()

        return step

    loop(1, ny, pass_on(r_out, r_across))
    loop(1, ny, pass_on(g_out, g_across))
    loop(0, ny, lambda k: r_across(k).wait_recv())
    loop(0, ny, lambda k: g_across(k).wait_recv())

    order = mp * rows
    g = gful[...].reshape(order, width)
    mine = gful[m]
    zb[0, z] = lax.dot_general(
        mine, g, (((1,), (1,)), ((), ())), preferred_element_type=f32
    ).astype(bf16)

    def ring(ch, h, way):
        if way == 0:
            at = (z + nz - (h - 1)) % nz
            return send(zb.at[ch, at], zb.at[ch, at], s_f.at[ch, way, h], r_f.at[ch, way, h], at_z(1))
        at = (z + (h - 1)) % nz
        return send(
            zb.at[ch, at], zb.at[ch, at], s_f.at[ch, way, h], r_f.at[ch, way, h], at_z(nz - 1)
        )

    hops = (nz // 2, nz - 1 - nz // 2)

    def ring_start(ch, h):
        for way in range(2):
            if h <= hops[way]:
                ring(ch, h, way).start()

    def ring_recv(ch, h):
        for way in range(2):
            if h <= hops[way]:
                ring(ch, h, way).wait_recv()

    ring_start(0, 1)
    piece = pl.multiple_of((m * rows // 128) * 128, 128)
    columns = gful[:, :, pl.ds(piece, 128)].reshape(order, 128)
    slab[...] = lax.dot_general(columns, g, (((0,), (0,)), ((), ())), preferred_element_type=f32)
    zb[1, z] = slab[pl.ds((m * rows) % 128, rows), :].astype(bf16)
    ring_start(1, 1)
    applied = jnp.dot(rz[source, 0], g, preferred_element_type=f32).astype(bf16)
    cond = jnp.dot(applied, rful[...].reshape(order, width), preferred_element_type=f32)
    cond_v[...] = cond
    partial_sum = jnp.broadcast_to(jnp.sum(cond * cond, keepdims=True), ssq_s.shape)
    ssq_s[...] = partial_sum
    ssq[m] = partial_sum

    def square_send(k):
        return send(ssq_s, ssq.at[m], s_q.at[k - 1], r_q.at[k - 1], at_m(k))

    loop(1, mp, lambda k: square_send(k).start())
    wide_g = g.astype(f32)
    grad_square = jnp.sum(wide_g * wide_g, keepdims=True)
    loop(1, mp, lambda k: square_send(k).wait_recv())
    cond_square = jnp.sum(ssq[...], axis=0)[0:1, 0:1]
    entries = float(order * width)
    ratio = jnp.sqrt((grad_square / entries + epsilon) / (cond_square / entries + epsilon))
    zb[2, z] = (cond_v[...] * ratio).astype(bf16)
    ring_start(2, 1)
    for h in range(1, hops[0] + 1):
        for ch in range(3):
            ring_recv(ch, h)
            if h < hops[0]:
                ring_start(ch, h + 1)

    def pick(col, place):
        o = z * COLS + col
        begin = tab[1, o]
        k = (begin + (x + 4 * COLS * nz - begin) % COLS) // COLS
        k = jnp.minimum(k, nz - 1)
        place[0] = zb[0, k]
        place[1] = zb[1, k]
        place[2] = zb[2, tab[0, o] // COLS]

    fin = []
    for k in range(1, COLS):
        pick((x + k) % COLS, fxs.at[k - 1])
        copy = send(fxs.at[k - 1], fx.at[x], s_fx.at[k - 1], r_fx.at[k - 1], at_x(k))
        copy.start()
        fin.append(copy)
    pick(x, fx.at[x])
    for copy in fin:
        copy.wait_recv()
    loads[4].wait()
    loads[5].wait()
    limit = tab[4, dp]
    for r in range(cap):
        col = (start_me + r) % COLS
        live = limit > r
        new_left[r] = ls_v[r] + jnp.where(live, fx[col, 0].astype(f32), 0.0)
        new_right[r] = rs_v[r] + jnp.where(live, fx[col, 1].astype(f32), 0.0)
    home = fx[tab[0, dp] % COLS, 2].astype(f32)
    upd[0] = jnp.where(tab[5, dp] > 0, home, 0.0).astype(bf16)

    for copy in root_x + relay + direct + onward + fin:
        copy.wait_send()
    loop(1, nz, lambda k: root_send(k).wait_send())
    loop(1, nz, lambda k: z_send(k).wait_send())
    loop(1, ny, lambda k: r_out(k).wait_send())
    loop(1, ny, lambda k: g_out(k).wait_send())
    loop(0, ny, lambda k: r_across(k).wait_send())
    loop(0, ny, lambda k: g_across(k).wait_send())
    loop(1, mp, lambda k: square_send(k).wait_send())
    for ch in range(3):
        for way in range(2):
            for h in range(1, hops[way] + 1):
                ring(ch, h, way).wait_send()


def tables(owner_map, owner_counts, capacity):
    blocks = owner_map.shape[0]
    ids = jnp.arange(blocks, dtype=jnp.int32)
    earlier = ids[None, :] < ids[:, None]
    same = owner_map[None, :] == owner_map[:, None]
    rank = jnp.sum((same & earlier).astype(jnp.int32), axis=1)
    before = jnp.sum((owner_map[None, :] < owner_map[:, None]).astype(jnp.int32), axis=1)
    place = before + rank
    begin = jnp.sum((owner_map[None, :] < ids[:, None]).astype(jnp.int32), axis=1)
    owned = jnp.sum((owner_map[None, :] == ids[:, None]).astype(jnp.int32), axis=1)
    limit = jnp.minimum(jnp.minimum(owned, owner_counts), capacity)
    held = jnp.sum(jnp.where(owner_map[:, None] == ids[None, :], owner_counts[None, :], 0), axis=1)
    live = ((rank < held) & (rank < capacity)).astype(jnp.int32)
    at = place[None, :] == ids[:, None]
    block_at = jnp.sum(jnp.where(at, ids[None, :], 0), axis=1)
    owner_at = jnp.sum(jnp.where(at, owner_map[None, :], 0), axis=1)
    return jnp.stack([place, begin, block_at, owner_at, limit, live])


def shards(acts, cot, lstat, rstat, lroot, rroot, owner_map, owner_counts):
    cap, rows, width = lstat.shape
    tok, own = acts.shape
    dw = cot.shape[1]
    devices, mp = lax.axis_size("dp"), lax.axis_size("mp")
    nz, ny = devices // COLS, mp // 2
    tab = tables(owner_map, owner_counts, cap)
    sizes = (nz, ny, mp, rows, width, cap)
    V, D = pltpu.VMEM, pltpu.SemaphoreType.DMA
    half = nz // 2

    def pieces(*lead):
        return V((*lead, rows, width), bf16)

    scratch = [
        V((tok, own), bf16),
        V((own, tok), bf16),
        V((tok, dw), bf16),
        V(lstat.shape, f32),
        V(rstat.shape, f32),
        V(lroot.shape, bf16),
        V(rroot.shape, bf16),
        pieces(own // rows, dw // width),
        pieces(COLS, nz),
        pieces(2, half),
        pieces(4, half),
        pieces(2, half),
        pieces(nz),
        pieces(nz - 1),
        pieces(mp),
        pieces(mp),
        pieces(COLS - 1, 2),
        pieces(COLS, 2),
        pieces(nz, 2),
        pieces(nz, 2),
        V((128, width), f32),
        V((rows, width), f32),
        V((8, 128), f32),
        V((mp, 8, 128), f32),
        pieces(3, nz),
        pieces(COLS - 1, 3),
        pieces(COLS, 3),
        D((6,)),
    ]
    for shape in [
        (COLS - 1,),
        (nz - 1,),
        (4,),
        (2,),
        (nz - 1,),
        (2, ny),
        (2, ny),
        (mp - 1,),
        (3, 2, nz),
        (COLS - 1,),
    ]:
        scratch += [D(shape), D(shape)]
    anywhere = pl.BlockSpec(memory_space=pl.ANY)
    vmem = pl.BlockSpec(memory_space=pltpu.VMEM)
    return pl.pallas_call(
        functools.partial(kernel, sizes),
        out_shape=(
            jax.ShapeDtypeStruct((1, rows, width), bf16),
            jax.ShapeDtypeStruct(lstat.shape, f32),
            jax.ShapeDtypeStruct(rstat.shape, f32),
        ),
        in_specs=[pl.BlockSpec(memory_space=pltpu.SMEM)] + [anywhere] * 6,
        out_specs=(vmem,) * 3,
        scratch_shapes=scratch,
        compiler_params=pltpu.CompilerParams(
            collective_id=0, has_side_effects=True, vmem_limit_bytes=40 << 20
        ),
        name="shampoo",
    )(tab, acts, cot, lstat, rstat, lroot, rroot)


def solution(mesh):
    in_specs = (
        P("dp", "mp"),
        P("dp", None),
        P("dp", "mp", None),
        P("dp", "mp", None),
        P("dp", "mp", None),
        P("dp", "mp", None),
        P(),
        P(),
    )
    out_specs = (P("dp", "mp", None), P("dp", "mp", None), P("dp", "mp", None))
    return jax.shard_map(shards, mesh=mesh, in_specs=in_specs, out_specs=out_specs, check_vma=False)
```

time: 198 us -> 90.8 us (0.46)
  the two profiles are of different devices: /device:TPU:1 before, /device:TPU:4 now
where the time goes in v1:
time: 90.8 us; the launch traced here: 90.5 us
  Pallas kernels  78.8 us (87%)
  local copies, waits for them, and re-layouts  8.57 us (9%)
  other arithmetic  2.42 us (3%)
    pallas_call x1, Pallas kernels, shards(): pl.pallas_call(functools.partial(kernel, sizes), out_shape=(jax.ShapeDtyp...  78.8 us
    unnamed x15, local copies, waits for them, and re-layouts  8.54 us

profile of v1, /device:TPU:4, one launch (start us, length us, event | category | flops | bytes accessed | tf_op | source)
XLA Modules:
  0.0 90.5 jit_solution(1519728593872058603)
XLA Ops:
  0.6 1.0 %select_reduce_fusion = (s32[32]{0:T(128)S(1)}, s32[32]{0:T(128)S(1)}, s32[32]{0:T(128)S(1)}, s32[32]{0:T(128)S(1)}, s32[32]{0:T(128)S(1)}) fusion(s32[32]{0:T(128)} %param.15, s32[32]{0:T(128)} %param.14), kind=kLoop, calls=%fused_computation | loop fusion | flops 17248 | bytes 896 | tf_op jit(solution)/shard_map/reduce_sum | solution.py:384
  1.6 0.7 minimum_bitcast_fusion
  2.3 0.8 select_reduce_fusion.1
  3.1 0.0 copy-start
  3.1 1.6 %copy-done = bf16[1024,1024]{1,0:T(8,128)(2,1)S(1)} copy-done((bf16[1024,1024]{1,0:T(8,128)(2,1)S(1)}, bf16[1024,1024]{1,0:T(8,128)(2,1)}, u32[]{:S(2)}) %copy-start) | copy-done | bytes 2097176
  4.7 0.0 copy-start.1
  4.7 1.2 %copy-done.1 = bf16[1024,512]{1,0:T(8,128)(2,1)S(1)} copy-done((bf16[1024,512]{1,0:T(8,128)(2,1)S(1)}, bf16[1024,512]{1,0:T(8,128)(2,1)}, u32[]{:S(2)}) %copy-start.1) | copy-done | bytes 1048600
  5.9 0.0 copy-start.2
  5.9 0.9 %copy-done.2 = f32[4,32,512]{2,1,0:T(8,128)S(1)} copy-done((f32[4,32,512]{2,1,0:T(8,128)S(1)}, f32[4,32,512]{2,1,0:T(8,128)}, u32[]{:S(2)}) %copy-start.2) | copy-done | bytes 262168
  6.9 0.0 copy-start.3
  6.9 0.9 %copy-done.3 = f32[4,32,512]{2,1,0:T(8,128)S(1)} copy-done((f32[4,32,512]{2,1,0:T(8,128)S(1)}, f32[4,32,512]{2,1,0:T(8,128)}, u32[]{:S(2)}) %copy-start.3) | copy-done | bytes 262168
  7.8 0.0 copy-start.4
  7.8 0.9 copy-done.4
  8.7 0.0 copy-start.5
  8.7 0.9 copy-done.5
  9.6 78.8 %shampoo.1 = (bf16[1,32,512]{2,1,0:T(8,128)(2,1)S(1)}, f32[4,32,512]{2,1,0:T(8,128)S(1)}, f32[4,32,512]{2,1,0:T(8,128)S(1)}) custom-call(s32[6,32]{1,0:T(8,128)S(1)} %stack.21.tab, bf16[1024,512]{1,0:T(8,128)(2,1)S(1)} %copy-done.1, bf16[1024,1024]{1,0:T(8,128)(2,1)S(1)} %copy-done, f32[4,32,512]{2,1,0:T(8,128)S(1)} %copy-done.2, ...), custom_call_target="tpu_custom_call" | custom-call | tf_op jit(solution)/shard_map/shampoo/pallas_call | solution.py:451
  88.4 0.6 copy.14
  89.0 0.7 copy.15
  89.8 0.7 copy.16
  (3 shorter events, 0.0 us)
Async XLA Ops:
  3.1 1.6 %copy-start = (bf16[1024,1024]{1,0:T(8,128)(2,1)S(1)}, bf16[1024,1024]{1,0:T(8,128)(2,1)}, u32[]{:S(2)}) copy-start(bf16[1024,1024]{1,0:T(8,128)(2,1)} %cot.1) | copy-start | bytes 6291460
  4.7 1.2 %copy-start.1 = (bf16[1024,512]{1,0:T(8,128)(2,1)S(1)}, bf16[1024,512]{1,0:T(8,128)(2,1)}, u32[]{:S(2)}) copy-start(bf16[1024,512]{1,0:T(8,128)(2,1)} %acts.1) | copy-start | bytes 3145732
  5.9 0.9 %copy-start.2 = (f32[4,32,512]{2,1,0:T(8,128)S(1)}, f32[4,32,512]{2,1,0:T(8,128)}, u32[]{:S(2)}) copy-start(f32[4,32,512]{2,1,0:T(8,128)} %lstat.1) | copy-start | bytes 786436
  6.9 0.9 %copy-start.3 = (f32[4,32,512]{2,1,0:T(8,128)S(1)}, f32[4,32,512]{2,1,0:T(8,128)}, u32[]{:S(2)}) copy-start(f32[4,32,512]{2,1,0:T(8,128)} %rstat.1) | copy-start | bytes 786436
  7.8 0.9 copy-start.4
  8.7 0.9 copy-start.5

commit v2 on v1

v2 whole, which is shorter than its diff:
```python
import functools

import jax
import jax.numpy as jnp
from jax import lax
from jax.experimental import pallas as pl
from jax.experimental.pallas import tpu as pltpu
from jax.sharding import PartitionSpec as P

epsilon = 1e-06
COLS = 4
MESH = pl.DeviceIdType.MESH
PLANS = {
    1: (),
    2: ((0, 0, 1, False),),
    4: ((0, 0, 1, True), (0, 0, 2, False)),
    8: ((0, 0, 1, True), (0, 0, 2, True), (1, 2, 1, True), (1, 2, 2, False)),
}
f32, bf16 = jnp.float32, jnp.bfloat16


def kernel(
    sizes,
    omap,
    counts,
    acts,
    cot,
    lstat,
    rstat,
    lroot,
    rroot,
    upd,
    new_left,
    new_right,
    tab_v,
    tab,
    a_v,
    at_v,
    c_v,
    ls_v,
    rs_v,
    lr_v,
    rr_v,
    part,
    q,
    rel,
    xa,
    fwd,
    xsum,
    zr,
    gful,
    rful,
    rxs,
    rx_l,
    rx_r,
    rzs,
    rz_l,
    rz_r,
    zrel,
    zfwd,
    slab,
    cond_v,
    ssq_s,
    ssq,
    zb_l,
    zb_r,
    zb_u,
    fxs,
    fxs_u,
    fx,
    fx_u,
    loc,
    s_rx,
    r_rx,
    s_rz,
    r_rz,
    s_x,
    r_x,
    s_z,
    r_z,
    s_y,
    r_y,
    s_c,
    r_c,
    s_q,
    r_q,
    s_f,
    r_f,
    s_fx,
    r_fx,
):
    nz, ny, mp, rows, width, cap = sizes
    dp = lax.axis_index("dp")
    m = lax.axis_index("mp")
    x, z = dp % COLS, dp // COLS
    c, y = m % 2, m // 2
    half = nz // 2
    rx, rz, zb = (rx_l, rx_r), (rz_l, rz_r), (zb_l, zb_r, zb_u)
    part_rows = [pl.ds(h * (rows // 2), rows // 2) for h in range(2)]

    def at_x(k):
        return {"dp": z * COLS + (x + k) % COLS}

    def at_z(k):
        return {"dp": ((z + k) % nz) * COLS + x}

    def at_y(k):
        return {"mp": ((y + k) % ny) * 2 + c}

    def at_m(k):
        return {"mp": (m + k) % mp}

    partner = {"mp": y * 2 + (1 - c)}

    def send(src, dst, ssem, rsem, where):
        return pltpu.make_async_remote_copy(
            src_ref=src,
            dst_ref=dst,
            send_sem=ssem,
            recv_sem=rsem,
            device_id=where,
            device_id_type=MESH,
        )

    def loop(lo, hi, body):
        def step(i, carry):
            body(i)
            return carry

        lax.fori_loop(lo, hi, step, 0)

    def spread(pos, n, where, ref, ssem, rsem):
        plan = PLANS[n]

        def copy(i, way):
            _, behind, hop, whole = plan[i]
            origin = (pos + n - behind) % n if way == 0 else (pos + behind) % n
            r = ref(origin, None if whole else way)
            return send(
                r, r, ssem.at[way, i], rsem.at[way, i], where(hop if way == 0 else n - hop)
            )

        def start(stage):
            for i, item in enumerate(plan):
                if item[0] == stage:
                    for way in range(2):
                        copy(i, way).start()

        def forward():
            if len(plan) > 2:
                for way in range(2):
                    copy(1, way).wait_recv()
                start(1)

        def finish(arrived=None):
            for i, item in enumerate(plan):
                for way in range(2):
                    if not (len(plan) > 2 and i == 1):
                        copy(i, way).wait_recv()
                if arrived is not None:
                    far = item[1] + item[2]
                    arrived(far)
                    if item[3]:
                        arrived(n - far)

        def drain():
            for i in range(len(plan)):
                for way in range(2):
                    copy(i, way).wait_send()

        return start, forward, finish, drain

    barrier = pltpu.get_barrier_semaphore()

    def hello(where):
        pl.semaphore_signal(barrier, inc=1, device_id=where, device_id_type=MESH)

    loads = [
        pltpu.make_async_copy(s, d, loc.at[i])
        for i, (s, d) in enumerate(
            [(lroot, lr_v), (rroot, rr_v), (acts, a_v), (cot, c_v), (lstat, ls_v), (rstat, rs_v)]
        )
    ]
    for i in (2, 3, 1, 0):
        loads[i].start()
    for k in range(1, COLS):
        hello(at_x(k))
    loop(1, nz, lambda k: hello(at_z(k)))
    loop(1, mp, lambda k: hello(at_m(k)))

    tables(omap, counts, cap, tab_v)
    to_scalars = pltpu.make_async_copy(tab_v, tab, loc.at[6])
    to_scalars.start()

    loads[2].wait()
    tiles = a_v.shape[1] // 128

    def turn(i):
        at_v[pl.ds(i * 128, 128), :] = a_v[:, pl.ds(pl.multiple_of(i * 128, 128), 128)].T

    loop(0, tiles, turn)
    loads[3].wait()
    wide = 256
    per = width // wide

    def multiply(n):
        got = jnp.dot(
            at_v[...],
            c_v[:, pl.ds(pl.multiple_of(n * wide, wide), wide)],
            preferred_element_type=f32,
        )
        got = got.astype(bf16).reshape(part.shape[0], rows, wide)
        part[:, n // per, :, pl.ds(pl.multiple_of((n % per) * wide, wide), wide)] = got

    loop(0, c_v.shape[1] // wide, multiply)
    ncol = c_v.shape[1] // width
    to_scalars.wait()

    def arrange(s):
        b = tab[2, s]
        q[s % COLS, s // COLS] = part[b // ncol, b % ncol]

    loop(0, COLS * nz, arrange)

    loads[0].wait()
    loads[1].wait()
    start_me = tab[1, dp]

    def slot_for(col):
        return (col + 4 * COLS * nz - start_me) % COLS

    for k in range(COLS):
        r = slot_for((x + k) % COLS)
        rxs[0, k] = lr_v[r]
        rxs[1, k] = rr_v[r]
    rx_l[x] = rxs[0, 0]
    rx_r[x] = rxs[1, 0]

    def root_x(which, k):
        return send(
            rxs.at[which, k], rx[which].at[x], s_rx.at[which, k], r_rx.at[which, k], at_x(k)
        )

    def root_z(which, k):
        return send(
            rzs.at[which, (z + k) % nz],
            rz[which].at[z],
            s_rz.at[which, k - 1],
            r_rz.at[which, k - 1],
            at_z(k),
        )

    def root_turn(which):
        for k in range(1, COLS):
            root_x(which, k).wait_recv()

        def root_row(k):
            row = (z + k) % nz
            rzs[which, row] = rx[which][tab[3, row * COLS + x] % COLS]

        loop(0, nz, root_row)
        rz[which][z] = rzs[which, z]
        loop(1, nz, lambda k: root_z(which, k).start())

    pl.semaphore_wait(barrier, COLS - 1 + nz - 1 + mp - 1)
    lo, hi = pl.ds(0, half), pl.ds(half, half)
    far, right, left = (x + 2) % COLS, (x + 1) % COLS, (x + 3) % COLS

    def x_copy(h, j, src, dst, k):
        return send(
            src.at[:, part_rows[h], :],
            dst.at[:, part_rows[h], :],
            s_x.at[h, j],
            r_x.at[h, j],
            at_x(k),
        )

    relay, direct, onward = [], [], []
    for h in range(2):
        relay.append(
            [
                x_copy(h, 0, q.at[far, lo], rel.at[0], 1),
                x_copy(h, 1, q.at[far, hi], rel.at[1], 3),
            ]
        )
        direct.append(
            [
                x_copy(h, 2, q.at[right, hi], xa.at[0], 1),
                x_copy(h, 3, q.at[left, lo], xa.at[1], 3),
            ]
        )
        onward.append(
            [x_copy(h, 4, fwd.at[0], xa.at[2], 1), x_copy(h, 5, fwd.at[1], xa.at[3], 3)]
        )
    for k in range(1, COLS):
        root_x(1, k).start()
    for copy in relay[0] + direct[0] + relay[1]:
        copy.start()

    def send_on(h):
        at = part_rows[h]
        for side, (toward, part_of) in enumerate([(right, lo), (left, hi)]):
            relay[h][side].wait_recv()
            fwd[side, :, at, :] = (
                q[toward, part_of, at, :].astype(f32) + rel[side, :, at, :].astype(f32)
            ).astype(bf16)
            onward[h][side].start()

    send_on(0)
    for copy in direct[1]:
        copy.start()
    root_turn(1)
    send_on(1)
    for k in range(1, COLS):
        root_x(0, k).start()

    def z_send(h, k):
        return send(
            xsum.at[(z + k) % nz, part_rows[h], :],
            zr.at[k - 1, part_rows[h], :],
            s_z.at[h, k - 1],
            r_z.at[h, k - 1],
            at_z(k),
        )

    def z_copy(h, way, kind):
        def there(k):
            return k if way == 0 else nz - k

        at = part_rows[h]
        cols = pl.ds(way * (width // 2), width // 2)
        j = 4 * way + kind
        if kind == 0:
            src, dst, k = xsum.at[(z + there(1)) % nz, at, :], zr.at[way, at, :], 1
        elif kind == 1:
            src, dst, k = xsum.at[(z + there(3)) % nz, at, :], zrel.at[way, 0, at, :], 1
        elif kind == 2:
            src, dst, k = xsum.at[(z + there(4)) % nz, at, cols], zrel.at[way, 1, at, cols], 2
        else:
            src, dst, k = zfwd.at[way, at, :], zr.at[2 + way, at, :], 2
        return send(src, dst, s_z.at[h, j], r_z.at[h, j], at_z(there(k)))

    def z_start(h):
        if nz != 8:
            loop(1, nz, lambda k: z_send(h, k).start())
            return
        for kind in (2, 1, 0):
            for way in range(2):
                z_copy(h, way, kind).start()

    def z_onward(h):
        if nz != 8:
            return
        at = part_rows[h]
        for way in range(2):
            cols = pl.ds(way * (width // 2), width // 2)
            z_copy(h, way, 1).wait_recv()
            z_copy(h, way, 2).wait_recv()
            to = (z + (2 if way == 0 else nz - 2)) % nz
            both = xsum[to, at, :].astype(f32) + zrel[way, 0, at, :].astype(f32)
            extra = zrel[way, 1, at, cols].astype(f32)
            none = jnp.zeros_like(extra)
            extra = jnp.concatenate([extra, none] if way == 0 else [none, extra], axis=1)
            zfwd[way, at, :] = (both + extra).astype(bf16)
            z_copy(h, way, 3).start()

    def z_finish(h):
        at = part_rows[h]
        total = xsum[z, at, :].astype(f32)
        if nz != 8:
            loop(1, nz, lambda k: z_send(h, k).wait_recv())
            for k in range(nz - 1):
                total = total + zr[k, at, :].astype(f32)
            return total
        for way in range(2):
            z_copy(h, way, 0).wait_recv()
            z_copy(h, way, 3).wait_recv()
            total = total + zr[way, at, :].astype(f32) + zr[2 + way, at, :].astype(f32)
        return total

    def z_drain(h):
        if nz != 8:
            loop(1, nz, lambda k: z_send(h, k).wait_send())
            return
        for way in range(2):
            for kind in range(4):
                z_copy(h, way, kind).wait_send()

    def x_done(h):
        at = part_rows[h]
        for copy in direct[h] + onward[h]:
            copy.wait_recv()
        own = q[x, :, at, :].astype(f32)
        xsum[lo, at, :] = (
            own[:half] + xa[1, :, at, :].astype(f32) + xa[2, :, at, :].astype(f32)
        ).astype(bf16)
        xsum[hi, at, :] = (
            own[half:] + xa[0, :, at, :].astype(f32) + xa[3, :, at, :].astype(f32)
        ).astype(bf16)
        z_start(h)

    x_done(0)
    x_done(1)

    z_onward(0)
    loop(1, nz, lambda k: root_z(1, k).wait_recv())
    source = tab[3, dp] // COLS
    rful[m] = rz_r[source]

    def over_mp(full, j, at):
        def ref(origin, side):
            cols = slice(None) if side is None else pl.ds(side * (width // 2), width // 2)
            return full.at[origin * 2 + c, at, cols]

        def across(k):
            r = ref((y + ny - k) % ny, None)
            return send(r, r, s_c.at[j, k], r_c.at[j, k], partner)

        return spread(y, ny, at_y, ref, s_y.at[j], r_y.at[j]), across

    (r_start, r_forward, r_finish, r_drain), r_across = over_mp(rful, 2, pl.ds(0, rows))
    g_over = [over_mp(gful, h, part_rows[h]) for h in range(2)]
    r_start(0)
    r_across(0).start()
    z_onward(1)
    root_turn(0)

    def z_done(h):
        gful[m, part_rows[h], :] = z_finish(h).astype(bf16)
        (start, _, _, _), across = g_over[h]
        start(0)
        across(0).start()

    z_done(0)
    r_forward()
    z_done(1)
    g_over[0][0][1]()
    r_finish(lambda k: r_across(k).start())
    g_over[1][0][1]()
    for h in range(2):
        (_, _, finish, _), across = g_over[h]
        finish(lambda k, across=across: across(k).start())
    for _, across in g_over:
        loop(0, ny, lambda k, across=across: across(k).wait_recv())
    loop(0, ny, lambda k: r_across(k).wait_recv())
    loop(1, nz, lambda k: root_z(0, k).wait_recv())

    order = mp * rows
    g = gful[...].reshape(order, width)
    applied = jnp.dot(rz_l[source], g, preferred_element_type=f32).astype(bf16)
    cond = jnp.dot(applied, rful[...].reshape(order, width), preferred_element_type=f32)
    cond_v[...] = cond
    partial_sum = jnp.broadcast_to(jnp.sum(cond * cond, keepdims=True), ssq_s.shape)
    ssq_s[...] = partial_sum
    ssq[m] = partial_sum

    def square_send(k):
        return send(ssq_s, ssq.at[m], s_q.at[k - 1], r_q.at[k - 1], at_m(k))

    loop(1, mp, lambda k: square_send(k).start())

    z_over = [
        spread(z, nz, at_z, lambda o, side, b=b: b.at[o] if side is None else b.at[o, :, pl.ds(side * (width // 2), width // 2)], s_f.at[i], r_f.at[i])
        for i, b in enumerate(zb)
    ]

    mine = gful[m]
    zb_l[z] = lax.dot_general(
        mine, g, (((1,), (1,)), ((), ())), preferred_element_type=f32
    ).astype(bf16)
    z_over[0][0](0)
    piece = pl.multiple_of((m * rows // 128) * 128, 128)
    columns = gful[:, :, pl.ds(piece, 128)].reshape(order, 128)
    slab[...] = lax.dot_general(columns, g, (((0,), (0,)), ((), ())), preferred_element_type=f32)
    zb_r[z] = slab[pl.ds((m * rows) % 128, rows), :].astype(bf16)
    z_over[1][0](0)
    wide_g = g.astype(f32)
    grad_square = jnp.sum(wide_g * wide_g, keepdims=True)
    loads[4].start()
    loads[5].start()
    z_over[0][1]()
    loop(1, mp, lambda k: square_send(k).wait_recv())
    cond_square = jnp.sum(ssq[...], axis=0)[0:1, 0:1]
    entries = float(order * width)
    ratio = jnp.sqrt((grad_square / entries + epsilon) / (cond_square / entries + epsilon))
    zb_u[z] = (cond_v[...] * ratio).astype(bf16)
    z_over[2][0](0)
    z_over[1][1]()
    z_over[2][1]()
    z_over[0][2]()
    z_over[1][2]()

    def pick(col, place):
        begin = tab[1, z * COLS + col]
        k = (begin + (x + 4 * COLS * nz - begin) % COLS) // COLS
        k = jnp.minimum(k, nz - 1)
        place[0] = zb_l[k]
        place[1] = zb_r[k]

    def fin(j, k):
        src = fxs.at[k - 1] if j == 0 else fxs_u.at[k - 1]
        dst = fx.at[x] if j == 0 else fx_u.at[x]
        return send(src, dst, s_fx.at[j, k - 1], r_fx.at[j, k - 1], at_x(k))

    def pick_update(col):
        return zb_u[tab[0, z * COLS + col] // COLS]

    for k in (2, 1, 3):
        pick((x + k) % COLS, fxs.at[k - 1])
        fin(0, k).start()
    pick(x, fx.at[x])
    z_over[2][2]()
    for k in (2, 1, 3):
        fxs_u[k - 1] = pick_update((x + k) % COLS)
        fin(1, k).start()
    fx_u[x] = pick_update(x)
    for h in range(2):
        for copy in relay[h] + direct[h] + onward[h]:
            copy.wait_send()
        z_drain(h)
        g_over[h][0][3]()
        loop(0, ny, lambda k, h=h: g_over[h][1](k).wait_send())
        loop(1, nz, lambda k, h=h: root_z(h, k).wait_send())
        for k in range(1, COLS):
            root_x(h, k).wait_send()
    r_drain()
    loop(0, ny, lambda k: r_across(k).wait_send())
    loop(1, mp, lambda k: square_send(k).wait_send())
    for over in z_over:
        over[3]()
    for k in range(1, COLS):
        fin(0, k).wait_recv()
    loads[4].wait()
    loads[5].wait()
    limit = tab[4, dp]
    for r in range(cap):
        col = (start_me + r) % COLS
        live = limit > r
        new_left[r] = ls_v[r] + jnp.where(live, fx[col, 0].astype(f32), 0.0)
        new_right[r] = rs_v[r] + jnp.where(live, fx[col, 1].astype(f32), 0.0)
    for k in range(1, COLS):
        fin(1, k).wait_recv()
    home = fx_u[tab[0, dp] % COLS].astype(f32)
    upd[0] = jnp.where(tab[5, dp] > 0, home, 0.0).astype(bf16)
    for j in range(2):
        for k in range(1, COLS):
            fin(j, k).wait_send()


def tables(omap, counts, capacity, out):
    blocks = omap.shape[1]
    shape = (blocks, blocks)
    i = lax.broadcasted_iota(jnp.int32, shape, 0)
    j = lax.broadcasted_iota(jnp.int32, shape, 1)

    def over_i(value):
        return jnp.sum(value.astype(jnp.int32), axis=0, keepdims=True)

    def over_j(value):
        return jnp.sum(value.astype(jnp.int32), axis=1, keepdims=True)

    row = jnp.broadcast_to(omap[...], shape)
    many = jnp.broadcast_to(counts[...], shape)
    col = jnp.broadcast_to(over_j(jnp.where(i == j, row, 0)), shape)
    many_col = jnp.broadcast_to(over_j(jnp.where(i == j, many, 0)), shape)
    rank = over_i(jnp.where((col == row) & (i < j), 1, 0))
    place = over_i(jnp.where(col < row, 1, 0)) + rank
    place_col = over_j(jnp.where((row < col) | ((row == col) & (j < i)), 1, 0))
    at = jnp.broadcast_to(place_col, shape) == j
    limit = jnp.minimum(over_i(jnp.where(col == j, 1, 0)), counts[...])
    held = over_i(jnp.where(row == i, many_col, 0))
    live = jnp.where((rank < held) & (rank < capacity), 1, 0)
    for n, value in enumerate(
        [
            place,
            over_i(jnp.where(col < j, 1, 0)),
            over_i(jnp.where(at, i, 0)),
            over_i(jnp.where(at, col, 0)),
            jnp.minimum(limit, capacity),
            live,
        ]
    ):
        out[n : n + 1, 0:blocks] = value


def shards(acts, cot, lstat, rstat, lroot, rroot, owner_map, owner_counts):
    cap, rows, width = lstat.shape
    tok, own = acts.shape
    dw = cot.shape[1]
    devices, mp = lax.axis_size("dp"), lax.axis_size("mp")
    nz, ny = devices // COLS, mp // 2
    sizes = (nz, ny, mp, rows, width, cap)
    V, D = pltpu.VMEM, pltpu.SemaphoreType.DMA
    half = nz // 2

    def pieces(*lead):
        return V((*lead, rows, width), bf16)

    scratch = [
        V((8, 128), jnp.int32),
        pltpu.SMEM((8, 128), jnp.int32),
        V((tok, own), bf16),
        V((own, tok), bf16),
        V((tok, dw), bf16),
        V(lstat.shape, f32),
        V(rstat.shape, f32),
        V(lroot.shape, bf16),
        V(rroot.shape, bf16),
        pieces(own // rows, dw // width),
        pieces(COLS, nz),
        pieces(2, half),
        pieces(4, half),
        pieces(2, half),
        pieces(nz),
        pieces(max(nz - 1, 4)),
        pieces(mp),
        pieces(mp),
        pieces(2, COLS),
        pieces(COLS),
        pieces(COLS),
        pieces(2, nz),
        pieces(nz),
        pieces(nz),
        pieces(2, 2),
        pieces(2),
        V((128, width), f32),
        V((rows, width), f32),
        V((8, 128), f32),
        V((mp, 8, 128), f32),
        pieces(nz),
        pieces(nz),
        pieces(nz),
        pieces(COLS - 1, 2),
        pieces(COLS - 1),
        pieces(COLS, 2),
        pieces(COLS),
        D((7,)),
    ]
    for shape in [
        (2, COLS),
        (2, nz - 1),
        (2, 6),
        (2, max(nz - 1, 8)),
        (3, 2, 4),
        (3, ny),
        (mp - 1,),
        (3, 2, 4),
        (2, COLS - 1),
    ]:
        scratch += [D(shape), D(shape)]
    anywhere = pl.BlockSpec(memory_space=pl.ANY)
    vmem = pl.BlockSpec(memory_space=pltpu.VMEM)
    return pl.pallas_call(
        functools.partial(kernel, sizes),
        out_shape=(
            jax.ShapeDtypeStruct((1, rows, width), bf16),
            jax.ShapeDtypeStruct(lstat.shape, f32),
            jax.ShapeDtypeStruct(rstat.shape, f32),
        ),
        in_specs=[vmem] * 2 + [anywhere] * 6,
        out_specs=(vmem,) * 3,
        scratch_shapes=scratch,
        compiler_params=pltpu.CompilerParams(collective_id=0, has_side_effects=True),
        name="shampoo",
    )(owner_map[None], owner_counts[None], acts, cot, lstat, rstat, lroot, rroot)


def solution(mesh):
    in_specs = (
        P("dp", "mp"),
        P("dp", None),
        P("dp", "mp", None),
        P("dp", "mp", None),
        P("dp", "mp", None),
        P("dp", "mp", None),
        P(),
        P(),
    )
    out_specs = (P("dp", "mp", None), P("dp", "mp", None), P("dp", "mp", None))
    return jax.shard_map(shards, mesh=mesh, in_specs=in_specs, out_specs=out_specs, check_vma=False)
```

time: 90.8 us -> 75.9 us (0.84)
  the two profiles are of different devices: /device:TPU:4 before, /device:TPU:1 now
where the time goes in v2:
time: 75.9 us; the launch traced here: 75.7 us
  Pallas kernels  70.3 us (93%)
  local copies, waits for them, and re-layouts  4.72 us (6%)
    pallas_call x1, Pallas kernels, shards(): pl.pallas_call(functools.partial(kernel, sizes), out_shape=(jax.ShapeDtyp...  70.3 us
    unnamed x3, local copies, waits for them, and re-layouts  4.72 us

profile of v2, /device:TPU:1, one launch (start us, length us, event | category | flops | bytes accessed | tf_op | source)
XLA Modules:
  0.0 75.7 jit_solution(9563754597672549)
XLA Ops:
  0.6 70.3 %shampoo.1 = (bf16[1,32,512]{2,1,0:T(8,128)(2,1)}, f32[4,32,512]{2,1,0:T(8,128)}, f32[4,32,512]{2,1,0:T(8,128)}) custom-call(s32[1,32]{1,0:T(1,128)} %bitcast.2, s32[1,32]{1,0:T(1,128)} %bitcast.3, bf16[1024,512]{1,0:T(8,128)(2,1)} %acts.1, bf16[1024,1024]{1,0:T(8,128)(2,1)} %cot.1, f32[4,32,512]{2,1,0:T(8,128)} %lstat.1, f32[4,32,512]{2,1,0:T(8,128)} %rstat.1, ...), custom_call_target="tpu_custom_call" | custom-call | tf_op jit(solution)/shard_map/shampoo/pallas_call | solution.py:653
  70.9 1.4 %copy.14 = bf16[1,32,512]{2,1,0:T(8,128)(2,1)} copy(bf16[1,32,512]{2,1,0:T(8,128)(2,1)} %get-tuple-element.6) | data formatting | bytes 65536
  72.3 1.7 %copy.15 = f32[4,32,512]{2,1,0:T(8,128)} copy(f32[4,32,512]{2,1,0:T(8,128)} %get-tuple-element.7) | data formatting | bytes 524288
  74.0 1.7 %copy.16 = f32[4,32,512]{2,1,0:T(8,128)} copy(f32[4,32,512]{2,1,0:T(8,128)} %get-tuple-element.8) | data formatting | bytes 524288

commit v3 on v2

--- a/solution.py
+++ b/solution.py
@@ -25,20 +25,16 @@
     counts,
     acts,
     cot,
-    lstat,
-    rstat,
     lroot,
     rroot,
-    upd,
-    new_left,
-    new_right,
+    result,
+    om_v,
+    ct_v,
     tab_v,
     tab,
     a_v,
     at_v,
     c_v,
-    ls_v,
-    rs_v,
     lr_v,
     rr_v,
     part,
@@ -66,9 +62,10 @@
     zb_r,
     zb_u,
     fxs,
-    fxs_u,
-    fx,
+    fx_l,
+    fx_r,
     fx_u,
+    packed,
     loc,
     s_rx,
     r_rx,
@@ -96,6 +93,7 @@
     c, y = m % 2, m // 2
     half = nz // 2
     rx, rz, zb = (rx_l, rx_r), (rz_l, rz_r), (zb_l, zb_r, zb_u)
+    fx = (fx_l, fx_r, fx_u)
     part_rows = [pl.ds(h * (rows // 2), rows // 2) for h in range(2)]
 
     def at_x(k):
@@ -178,50 +176,39 @@
     loads = [
         pltpu.make_async_copy(s, d, loc.at[i])
         for i, (s, d) in enumerate(
-            [(lroot, lr_v), (rroot, rr_v), (acts, a_v), (cot, c_v), (lstat, ls_v), (rstat, rs_v)]
+            [
+                (lroot, lr_v),
+                (rroot, rr_v),
+                (acts, a_v),
+                (cot, c_v),
+                (omap, om_v),
+                (counts, ct_v),
+            ]
         )
     ]
-    for i in (2, 3, 1, 0):
+    for i in (4, 5, 2, 3, 1, 0):
         loads[i].start()
     for k in range(1, COLS):
         hello(at_x(k))
     loop(1, nz, lambda k: hello(at_z(k)))
     loop(1, mp, lambda k: hello(at_m(k)))
 
-    tables(omap, counts, cap, tab_v)
+    loads[4].wait()
+    loads[5].wait()
+    tables(om_v, ct_v, cap, tab_v)
     to_scalars = pltpu.make_async_copy(tab_v, tab, loc.at[6])
     to_scalars.start()
 
     loads[2].wait()
     tiles = a_v.shape[1] // 128
+    each = 128 // rows
 
     def turn(i):
-        at_v[pl.ds(i * 128, 128), :] = a_v[:, pl.ds(pl.multiple_of(i * 128, 128), 128)].T
+        columns = a_v[:, pl.ds(pl.multiple_of(i * 128, 128), 128)]
+        at_v[pl.ds(i * each, each)] = columns.T.reshape(each, rows, a_v.shape[0])
 
     loop(0, tiles, turn)
-    loads[3].wait()
-    wide = 256
-    per = width // wide
-
-    def multiply(n):
-        got = jnp.dot(
-            at_v[...],
-            c_v[:, pl.ds(pl.multiple_of(n * wide, wide), wide)],
-            preferred_element_type=f32,
-        )
-        got = got.astype(bf16).reshape(part.shape[0], rows, wide)
-        part[:, n // per, :, pl.ds(pl.multiple_of((n % per) * wide, wide), wide)] = got
-
-    loop(0, c_v.shape[1] // wide, multiply)
-    ncol = c_v.shape[1] // width
     to_scalars.wait()
-
-    def arrange(s):
-        b = tab[2, s]
-        q[s % COLS, s // COLS] = part[b // ncol, b % ncol]
-
-    loop(0, COLS * nz, arrange)
-
     loads[0].wait()
     loads[1].wait()
     start_me = tab[1, dp]
@@ -263,6 +250,34 @@
         loop(1, nz, lambda k: root_z(which, k).start())
 
     pl.semaphore_wait(barrier, COLS - 1 + nz - 1 + mp - 1)
+    for k in (2, 1, 3):
+        root_x(1, k).start()
+    loads[3].wait()
+
+    wide = 256
+    per = width // wide
+    ncol = c_v.shape[1] // width
+
+    def multiply(n):
+        got = jnp.dot(
+            at_v[...].reshape(-1, c_v.shape[0]),
+            c_v[:, pl.ds(pl.multiple_of(n * wide, wide), wide)],
+            preferred_element_type=f32,
+        )
+        got = got.astype(bf16).reshape(part.shape[0], rows, wide)
+        part[:, n // per, :, pl.ds(pl.multiple_of((n % per) * wide, wide), wide)] = got
+
+    def arrange(h):
+        at = part_rows[h]
+
+        def one(s):
+            b = tab[2, s]
+            q[s % COLS, s // COLS, at, :] = part[b // ncol, b % ncol, at, :]
+
+        loop(0, COLS * nz, one)
+
+    loop(0, c_v.shape[1] // wide, multiply)
+    arrange(0)
     lo, hi = pl.ds(0, half), pl.ds(half, half)
     far, right, left = (x + 2) % COLS, (x + 1) % COLS, (x + 3) % COLS
 
@@ -292,9 +307,10 @@
         onward.append(
             [x_copy(h, 4, fwd.at[0], xa.at[2], 1), x_copy(h, 5, fwd.at[1], xa.at[3], 3)]
         )
-    for k in range(1, COLS):
-        root_x(1, k).start()
-    for copy in relay[0] + direct[0] + relay[1]:
+    for copy in relay[0] + direct[0]:
+        copy.start()
+    arrange(1)
+    for copy in relay[1]:
         copy.start()
 
     def send_on(h):
@@ -435,8 +451,8 @@
     r_forward()
     z_done(1)
     g_over[0][0][1]()
+    g_over[1][0][1]()
     r_finish(lambda k: r_across(k).start())
-    g_over[1][0][1]()
     for h in range(2):
         (_, _, finish, _), across = g_over[h]
         finish(lambda k, across=across: across(k).start())
@@ -476,8 +492,6 @@
     z_over[1][0](0)
     wide_g = g.astype(f32)
     grad_square = jnp.sum(wide_g * wide_g, keepdims=True)
-    loads[4].start()
-    loads[5].start()
     z_over[0][1]()
     loop(1, mp, lambda k: square_send(k).wait_recv())
     cond_square = jnp.sum(ssq[...], axis=0)[0:1, 0:1]
@@ -486,34 +500,33 @@
     zb_u[z] = (cond_v[...] * ratio).astype(bf16)
     z_over[2][0](0)
     z_over[1][1]()
-    z_over[2][1]()
-    z_over[0][2]()
-    z_over[1][2]()
-
-    def pick(col, place):
+
+    def seat_row(col):
         begin = tab[1, z * COLS + col]
         k = (begin + (x + 4 * COLS * nz - begin) % COLS) // COLS
-        k = jnp.minimum(k, nz - 1)
-        place[0] = zb_l[k]
-        place[1] = zb_r[k]
+        return jnp.minimum(k, nz - 1)
 
     def fin(j, k):
-        src = fxs.at[k - 1] if j == 0 else fxs_u.at[k - 1]
-        dst = fx.at[x] if j == 0 else fx_u.at[x]
-        return send(src, dst, s_fx.at[j, k - 1], r_fx.at[j, k - 1], at_x(k))
-
-    def pick_update(col):
-        return zb_u[tab[0, z * COLS + col] // COLS]
-
-    for k in (2, 1, 3):
-        pick((x + k) % COLS, fxs.at[k - 1])
-        fin(0, k).start()
-    pick(x, fx.at[x])
+        return send(
+            fxs.at[j, k - 1], fx[j].at[x], s_fx.at[j, k - 1], r_fx.at[j, k - 1], at_x(k)
+        )
+
+    def go_on(j):
+        def pick(col):
+            return zb[j][seat_row(col) if j < 2 else tab[0, z * COLS + col] // COLS]
+
+        for k in (2, 1, 3):
+            fxs[j, k - 1] = pick((x + k) % COLS)
+            fin(j, k).start()
+        fx[j][x] = pick(x)
+
+    z_over[0][2]()
+    go_on(0)
+    z_over[2][1]()
+    z_over[1][2]()
+    go_on(1)
     z_over[2][2]()
-    for k in (2, 1, 3):
-        fxs_u[k - 1] = pick_update((x + k) % COLS)
-        fin(1, k).start()
-    fx_u[x] = pick_update(x)
+    go_on(2)
     for h in range(2):
         for copy in relay[h] + direct[h] + onward[h]:
             copy.wait_send()
@@ -528,23 +541,50 @@
     loop(1, mp, lambda k: square_send(k).wait_send())
     for over in z_over:
         over[3]()
-    for k in range(1, COLS):
-        fin(0, k).wait_recv()
-    loads[4].wait()
-    loads[5].wait()
     limit = tab[4, dp]
-    for r in range(cap):
-        col = (start_me + r) % COLS
-        live = limit > r
-        new_left[r] = ls_v[r] + jnp.where(live, fx[col, 0].astype(f32), 0.0)
-        new_right[r] = rs_v[r] + jnp.where(live, fx[col, 1].astype(f32), 0.0)
-    for k in range(1, COLS):
-        fin(1, k).wait_recv()
-    home = fx_u[tab[0, dp] % COLS].astype(f32)
-    upd[0] = jnp.where(tab[5, dp] > 0, home, 0.0).astype(bf16)
+
+    def put(j):
+        at = pl.ds(j * cap, cap if j < 2 else 1)
+        return pltpu.make_async_copy(packed.at[at], result.at[at], loc.at[7 + j])
+
     for j in range(2):
         for k in range(1, COLS):
+            fin(j, k).wait_recv()
+        for r in range(cap):
+            add = fx[j][(start_me + r) % COLS]
+            packed[j * cap + r] = jnp.where(limit > r, add, jnp.zeros_like(add))
+        put(j).start()
+    for k in range(1, COLS):
+        fin(2, k).wait_recv()
+    home = fx[2][tab[0, dp] % COLS]
+    packed[2 * cap] = jnp.where(tab[5, dp] > 0, home, jnp.zeros_like(home))
+    put(2).start()
+    for j in range(3):
+        for k in range(1, COLS):
             fin(j, k).wait_send()
+    for j in range(3):
+        put(j).wait()
+
+
+def finish(result, lstat, rstat, upd, new_left, new_right, packed, old, new, loc, out):
+    cap = old.shape[1]
+    get = [
+        pltpu.make_async_copy(s, d, loc.at[i])
+        for i, (s, d) in enumerate([(result, packed), (lstat, old.at[0]), (rstat, old.at[1])])
+    ]
+    for copy in get:
+        copy.start()
+    get[0].wait()
+    put = [pltpu.make_async_copy(packed.at[pl.ds(2 * cap, 1)], upd, out.at[0])]
+    put[0].start()
+    for j, to in enumerate([new_left, new_right]):
+        get[1 + j].wait()
+        new[j] = old[j] + packed[pl.ds(j * cap, cap)].astype(f32)
+        copy = pltpu.make_async_copy(new.at[j], to, out.at[1 + j])
+        copy.start()
+        put.append(copy)
+    for copy in put:
+        copy.wait()
 
 
 def tables(omap, counts, capacity, out):
@@ -597,13 +637,13 @@
         return V((*lead, rows, width), bf16)
 
     scratch = [
+        V((1, devices), jnp.int32),
+        V((1, devices), jnp.int32),
         V((8, 128), jnp.int32),
         pltpu.SMEM((8, 128), jnp.int32),
         V((tok, own), bf16),
-        V((own, tok), bf16),
+        V((own // rows, rows, tok), bf16),
         V((tok, dw), bf16),
-        V(lstat.shape, f32),
-        V(rstat.shape, f32),
         V(lroot.shape, bf16),
         V(rroot.shape, bf16),
         pieces(own // rows, dw // width),
@@ -630,11 +670,12 @@
         pieces(nz),
         pieces(nz),
         pieces(nz),
-        pieces(COLS - 1, 2),
-        pieces(COLS - 1),
-        pieces(COLS, 2),
+        pieces(3, COLS - 1),
         pieces(COLS),
-        D((7,)),
+        pieces(COLS),
+        pieces(COLS),
+        pieces(2 * cap + 1),
+        D((10,)),
     ]
     for shape in [
         (2, COLS),
@@ -645,24 +686,37 @@
         (3, ny),
         (mp - 1,),
         (3, 2, 4),
-        (2, COLS - 1),
+        (3, COLS - 1),
     ]:
         scratch += [D(shape), D(shape)]
-    anywhere = pl.BlockSpec(memory_space=pl.ANY)
-    vmem = pl.BlockSpec(memory_space=pltpu.VMEM)
+    anywhere = pl.BlockSpec(memory_space=pltpu.HBM)
+    result = pl.pallas_call(
+        functools.partial(kernel, sizes),
+        out_shape=jax.ShapeDtypeStruct((2 * cap + 1, rows, width), bf16),
+        in_specs=[anywhere] * 6,
+        out_specs=anywhere,
+        scratch_shapes=scratch,
+        compiler_params=pltpu.CompilerParams(collective_id=0, has_side_effects=True),
+        name="shampoo",
+    )(owner_map[None], owner_counts[None], acts, cot, lroot, rroot)
     return pl.pallas_call(
-        functools.partial(kernel, sizes),
+        finish,
         out_shape=(
             jax.ShapeDtypeStruct((1, rows, width), bf16),
             jax.ShapeDtypeStruct(lstat.shape, f32),
             jax.ShapeDtypeStruct(rstat.shape, f32),
         ),
-        in_specs=[vmem] * 2 + [anywhere] * 6,
-        out_specs=(vmem,) * 3,
-        scratch_shapes=scratch,
-        compiler_params=pltpu.CompilerParams(collective_id=0, has_side_effects=True),
-        name="shampoo",
-    )(owner_map[None], owner_counts[None], acts, cot, lstat, rstat, lroot, rroot)
+        in_specs=[anywhere] * 3,
+        out_specs=(anywhere,) * 3,
+        scratch_shapes=[
+            pieces(2 * cap + 1),
+            V((2, *lstat.shape), f32),
+            V((2, *lstat.shape), f32),
+            D((3,)),
+            D((3,)),
+        ],
+        name="finish",
+    )(result, lstat, rstat)
 
 
 def solution(mesh):

time: 75.9 us -> 72.5 us (0.955)
  local copies, waits for them, and re-layouts: 4.72 us -> 0 us
  Pallas kernels: 70.3 us -> 71.7 us
    unnamed x3 -> x0, local copies, waits for them, and re-layouts: 4.72 us -> none
    pallas_call x1 -> x2, Pallas kernels: 70.3 us -> 71.7 us  [the longest x1 69.8 us: shards(): pl.pallas_call(functools.partial(kernel, sizes), out_shape=jax.ShapeDtype...]
where the time goes in v3:
time: 72.5 us; the launch traced here: 72.3 us
  Pallas kernels  71.7 us (99%)
    pallas_call x1, Pallas kernels, shards(): pl.pallas_call(functools.partial(kernel, sizes), out_shape=jax.ShapeDtype...  69.8 us
    pallas_call x1, Pallas kernels, shards(): pl.pallas_call(finish, out_shape=(jax.ShapeDtypeStruct((1, rows, width),...  1.9 us

profile of v3, /device:TPU:1, one launch (start us, length us, event | category | flops | bytes accessed | tf_op | source)
XLA Modules:
  0.0 72.3 jit_solution(5721028916066409735)
XLA Ops:
  0.6 69.8 %shampoo.1.result = bf16[9,32,512]{2,1,0:T(8,128)(2,1)} custom-call(s32[1,32]{1,0:T(1,128)} %bitcast.2, s32[1,32]{1,0:T(1,128)} %bitcast.3, bf16[1024,512]{1,0:T(8,128)(2,1)} %acts.1, bf16[1024,1024]{1,0:T(8,128)(2,1)} %cot.1, bf16[4,32,512]{2,1,0:T(8,128)(2,1)} %lroot.1, bf16[4,32,512]{2,1,0:T(8,128)(2,1)} %rroot.1), custom_call_target="tpu_custom_call" | custom-call | tf_op jit(solution)/shard_map/shampoo/pallas_call | solution.py:693
  70.4 1.9 %finish.1 = (bf16[1,32,512]{2,1,0:T(8,128)(2,1)}, f32[4,32,512]{2,1,0:T(8,128)}, f32[4,32,512]{2,1,0:T(8,128)}) custom-call(bf16[9,32,512]{2,1,0:T(8,128)(2,1)} %shampoo.1.result, f32[4,32,512]{2,1,0:T(8,128)} %lstat.1, f32[4,32,512]{2,1,0:T(8,128)} %rstat.1), custom_call_target="tpu_custom_call" | custom-call | tf_op jit(solution)/shard_map/finish/pallas_call | solution.py:702

commit v4 on v3

--- a/solution.py
+++ b/solution.py
@@ -49,15 +49,23 @@
     rxs,
     rx_l,
     rx_r,
-    rzs,
     rz_l,
     rz_r,
+    rel_l,
+    rel_r,
+    fwd_l,
+    fwd_r,
+    got_l,
+    got_r,
     zrel,
     zfwd,
     slab,
-    cond_v,
     ssq_s,
     ssq,
+    ratio_s,
+    ratio_z,
+    ratio_xs,
+    ratio_x,
     zb_l,
     zb_r,
     zb_u,
@@ -69,8 +77,6 @@
     loc,
     s_rx,
     r_rx,
-    s_rz,
-    r_rz,
     s_x,
     r_x,
     s_z,
@@ -85,6 +91,8 @@
     r_f,
     s_fx,
     r_fx,
+    s_t,
+    r_t,
 ):
     nz, ny, mp, rows, width, cap = sizes
     dp = lax.axis_index("dp")
@@ -209,6 +217,85 @@
 
     loop(0, tiles, turn)
     to_scalars.wait()
+    def sum_z(src, near, fwd_z, got, n, at):
+        def plain(k):
+            return send(
+                src.at[(z + k) % nz, at, :],
+                got.at[k - 1, at, :],
+                s_z.at[n, k - 1],
+                r_z.at[n, k - 1],
+                at_z(k),
+            )
+
+        def copy(way, kind):
+            def there(k):
+                return k if way == 0 else nz - k
+
+            cols = pl.ds(way * (width // 2), width // 2)
+            if kind == 0:
+                a, b, k = src.at[(z + there(1)) % nz, at, :], got.at[way, at, :], 1
+            elif kind == 1:
+                a, b, k = src.at[(z + there(3)) % nz, at, :], near.at[way, 0, at, :], 1
+            elif kind == 2:
+                a, b, k = src.at[(z + there(4)) % nz, at, cols], near.at[way, 1, at, cols], 2
+            else:
+                a, b, k = fwd_z.at[way, at, :], got.at[2 + way, at, :], 2
+            j = 4 * way + kind
+            return send(a, b, s_z.at[n, j], r_z.at[n, j], at_z(there(k)))
+
+        def start():
+            if nz != 8:
+                loop(1, nz, lambda k: plain(k).start())
+                return
+            for kind in (2, 1, 0):
+                for way in range(2):
+                    copy(way, kind).start()
+
+        def onward():
+            if nz != 8:
+                return
+            for way in range(2):
+                cols = pl.ds(way * (width // 2), width // 2)
+                copy(way, 1).wait_recv()
+                copy(way, 2).wait_recv()
+                to = (z + (2 if way == 0 else nz - 2)) % nz
+                both = src[to, at, :].astype(f32) + near[way, 0, at, :].astype(f32)
+                extra = near[way, 1, at, cols].astype(f32)
+                none = jnp.zeros_like(extra)
+                extra = jnp.concatenate([extra, none] if way == 0 else [none, extra], axis=1)
+                fwd_z[way, at, :] = (both + extra).astype(bf16)
+                copy(way, 3).start()
+
+        def finish_z():
+            total = src[z, at, :].astype(f32)
+            if nz != 8:
+                loop(1, nz, lambda k: plain(k).wait_recv())
+                for k in range(nz - 1):
+                    total = total + got[k, at, :].astype(f32)
+                return total
+            for way in range(2):
+                copy(way, 0).wait_recv()
+                copy(way, 3).wait_recv()
+                total = total + got[way, at, :].astype(f32) + got[2 + way, at, :].astype(f32)
+            return total
+
+        def drain():
+            if nz != 8:
+                loop(1, nz, lambda k: plain(k).wait_send())
+                return
+            for way in range(2):
+                for kind in range(4):
+                    copy(way, kind).wait_send()
+
+        return start, onward, finish_z, drain
+
+    grad_z = [sum_z(xsum, zrel, zfwd, zr, h, part_rows[h]) for h in range(2)]
+    every = pl.ds(0, rows)
+    root_z = [
+        sum_z(rz_l, rel_l, fwd_l, got_l, 2, every),
+        sum_z(rz_r, rel_r, fwd_r, got_r, 3, every),
+    ]
+
     loads[0].wait()
     loads[1].wait()
     start_me = tab[1, dp]
@@ -228,26 +315,17 @@
             rxs.at[which, k], rx[which].at[x], s_rx.at[which, k], r_rx.at[which, k], at_x(k)
         )
 
-    def root_z(which, k):
-        return send(
-            rzs.at[which, (z + k) % nz],
-            rz[which].at[z],
-            s_rz.at[which, k - 1],
-            r_rz.at[which, k - 1],
-            at_z(k),
-        )
-
     def root_turn(which):
         for k in range(1, COLS):
             root_x(which, k).wait_recv()
 
-        def root_row(k):
-            row = (z + k) % nz
-            rzs[which, row] = rx[which][tab[3, row * COLS + x] % COLS]
+        def root_row(row):
+            owner = tab[3, row * COLS + x]
+            block = rx[which][owner % COLS]
+            rz[which][row] = jnp.where(owner // COLS == z, block, jnp.zeros_like(block))
 
         loop(0, nz, root_row)
-        rz[which][z] = rzs[which, z]
-        loop(1, nz, lambda k: root_z(which, k).start())
+        root_z[which][0]()
 
     pl.semaphore_wait(barrier, COLS - 1 + nz - 1 + mp - 1)
     for k in (2, 1, 3):
@@ -274,7 +352,11 @@
             b = tab[2, s]
             q[s % COLS, s // COLS, at, :] = part[b // ncol, b % ncol, at, :]
 
-        loop(0, COLS * nz, one)
+        def row(k):
+            for col in range(COLS):
+                one(k * COLS + col)
+
+        loop(0, nz, row)
 
     loop(0, c_v.shape[1] // wide, multiply)
     arrange(0)
@@ -322,85 +404,13 @@
             ).astype(bf16)
             onward[h][side].start()
 
+    root_turn(1)
     send_on(0)
     for copy in direct[1]:
         copy.start()
-    root_turn(1)
     send_on(1)
     for k in range(1, COLS):
         root_x(0, k).start()
-
-    def z_send(h, k):
-        return send(
-            xsum.at[(z + k) % nz, part_rows[h], :],
-            zr.at[k - 1, part_rows[h], :],
-            s_z.at[h, k - 1],
-            r_z.at[h, k - 1],
-            at_z(k),
-        )
-
-    def z_copy(h, way, kind):
-        def there(k):
-            return k if way == 0 else nz - k
-
-        at = part_rows[h]
-        cols = pl.ds(way * (width // 2), width // 2)
-        j = 4 * way + kind
-        if kind == 0:
-            src, dst, k = xsum.at[(z + there(1)) % nz, at, :], zr.at[way, at, :], 1
-        elif kind == 1:
-            src, dst, k = xsum.at[(z + there(3)) % nz, at, :], zrel.at[way, 0, at, :], 1
-        elif kind == 2:
-            src, dst, k = xsum.at[(z + there(4)) % nz, at, cols], zrel.at[way, 1, at, cols], 2
-        else:
-            src, dst, k = zfwd.at[way, at, :], zr.at[2 + way, at, :], 2
-        return send(src, dst, s_z.at[h, j], r_z.at[h, j], at_z(there(k)))
-
-    def z_start(h):
-        if nz != 8:
-            loop(1, nz, lambda k: z_send(h, k).start())
-            return
-        for kind in (2, 1, 0):
-            for way in range(2):
-                z_copy(h, way, kind).start()
-
-    def z_onward(h):
-        if nz != 8:
-            return
-        at = part_rows[h]
-        for way in range(2):
-            cols = pl.ds(way * (width // 2), width // 2)
-            z_copy(h, way, 1).wait_recv()
-            z_copy(h, way, 2).wait_recv()
-            to = (z + (2 if way == 0 else nz - 2)) % nz
-            both = xsum[to, at, :].astype(f32) + zrel[way, 0, at, :].astype(f32)
-            extra = zrel[way, 1, at, cols].astype(f32)
-            none = jnp.zeros_like(extra)
-            extra = jnp.concatenate([extra, none] if way == 0 else [none, extra], axis=1)
-            zfwd[way, at, :] = (both + extra).astype(bf16)
-            z_copy(h, way, 3).start()
-
-    def z_finish(h):
-        at = part_rows[h]
-        total = xsum[z, at, :].astype(f32)
-        if nz != 8:
-            loop(1, nz, lambda k: z_send(h, k).wait_recv())
-            for k in range(nz - 1):
-                total = total + zr[k, at, :].astype(f32)
-            return total
-        for way in range(2):
-            z_copy(h, way, 0).wait_recv()
-            z_copy(h, way, 3).wait_recv()
-            total = total + zr[way, at, :].astype(f32) + zr[2 + way, at, :].astype(f32)
-        return total
-
-    def z_drain(h):
-        if nz != 8:
-            loop(1, nz, lambda k: z_send(h, k).wait_send())
-            return
-        for way in range(2):
-            for kind in range(4):
-                z_copy(h, way, kind).wait_send()
 
     def x_done(h):
         at = part_rows[h]
@@ -413,15 +423,14 @@
         xsum[hi, at, :] = (
             own[half:] + xa[0, :, at, :].astype(f32) + xa[3, :, at, :].astype(f32)
         ).astype(bf16)
-        z_start(h)
-
+        grad_z[h][0]()
+
+    root_z[1][1]()
     x_done(0)
     x_done(1)
 
-    z_onward(0)
-    loop(1, nz, lambda k: root_z(1, k).wait_recv())
-    source = tab[3, dp] // COLS
-    rful[m] = rz_r[source]
+    grad_z[0][1]()
+    rful[m] = root_z[1][2]().astype(bf16)
 
     def over_mp(full, j, at):
         def ref(origin, side):
@@ -438,11 +447,11 @@
     g_over = [over_mp(gful, h, part_rows[h]) for h in range(2)]
     r_start(0)
     r_across(0).start()
-    z_onward(1)
+    grad_z[1][1]()
     root_turn(0)
 
     def z_done(h):
-        gful[m, part_rows[h], :] = z_finish(h).astype(bf16)
+        gful[m, part_rows[h], :] = grad_z[h][2]().astype(bf16)
         (start, _, _, _), across = g_over[h]
         start(0)
         across(0).start()
@@ -451,6 +460,7 @@
     r_forward()
     z_done(1)
     g_over[0][0][1]()
+    root_z[0][1]()
     g_over[1][0][1]()
     r_finish(lambda k: r_across(k).start())
     for h in range(2):
@@ -459,26 +469,27 @@
     for _, across in g_over:
         loop(0, ny, lambda k, across=across: across(k).wait_recv())
     loop(0, ny, lambda k: r_across(k).wait_recv())
-    loop(1, nz, lambda k: root_z(0, k).wait_recv())
-
-    order = mp * rows
-    g = gful[...].reshape(order, width)
-    applied = jnp.dot(rz_l[source], g, preferred_element_type=f32).astype(bf16)
-    cond = jnp.dot(applied, rful[...].reshape(order, width), preferred_element_type=f32)
-    cond_v[...] = cond
-    partial_sum = jnp.broadcast_to(jnp.sum(cond * cond, keepdims=True), ssq_s.shape)
-    ssq_s[...] = partial_sum
-    ssq[m] = partial_sum
-
-    def square_send(k):
-        return send(ssq_s, ssq.at[m], s_q.at[k - 1], r_q.at[k - 1], at_m(k))
-
-    loop(1, mp, lambda k: square_send(k).start())
+    left_root = root_z[0][2]().astype(bf16)
 
     z_over = [
         spread(z, nz, at_z, lambda o, side, b=b: b.at[o] if side is None else b.at[o, :, pl.ds(side * (width // 2), width // 2)], s_f.at[i], r_f.at[i])
         for i, b in enumerate(zb)
     ]
+
+    order = mp * rows
+    g = gful[...].reshape(order, width)
+    applied = jnp.dot(left_root, g, preferred_element_type=f32).astype(bf16)
+    cond = jnp.dot(applied, rful[...].reshape(order, width), preferred_element_type=f32)
+    zb_u[z] = cond.astype(bf16)
+    z_over[2][0](0)
+    partial_sum = jnp.broadcast_to(jnp.sum(cond * cond, keepdims=True), ssq_s.shape)
+    ssq_s[...] = partial_sum
+    ssq[m] = partial_sum
+
+    def square_send(k):
+        return send(ssq_s, ssq.at[m], s_q.at[k - 1], r_q.at[k - 1], at_m(k))
+
+    loop(1, mp, lambda k: square_send(k).start())
 
     mine = gful[m]
     zb_l[z] = lax.dot_general(
@@ -492,13 +503,24 @@
     z_over[1][0](0)
     wide_g = g.astype(f32)
     grad_square = jnp.sum(wide_g * wide_g, keepdims=True)
+    z_over[2][1]()
     z_over[0][1]()
     loop(1, mp, lambda k: square_send(k).wait_recv())
     cond_square = jnp.sum(ssq[...], axis=0)[0:1, 0:1]
     entries = float(order * width)
     ratio = jnp.sqrt((grad_square / entries + epsilon) / (cond_square / entries + epsilon))
-    zb_u[z] = (cond_v[...] * ratio).astype(bf16)
-    z_over[2][0](0)
+    ratio_s[...] = jnp.broadcast_to(ratio, ratio_s.shape)
+    ratio_z[z] = jnp.broadcast_to(ratio, ratio_s.shape)
+
+    def ratio_up(k):
+        return send(ratio_s, ratio_z.at[z], s_t.at[0, k - 1], r_t.at[0, k - 1], at_z(k))
+
+    def ratio_on(k):
+        return send(
+            ratio_xs.at[k - 1], ratio_x.at[x], s_t.at[1, k - 1], r_t.at[1, k - 1], at_x(k)
+        )
+
+    loop(1, nz, lambda k: ratio_up(k).start())
     z_over[1][1]()
 
     def seat_row(col):
@@ -520,20 +542,19 @@
             fin(j, k).start()
         fx[j][x] = pick(x)
 
+    z_over[2][2]()
+    go_on(2)
     z_over[0][2]()
     go_on(0)
-    z_over[2][1]()
     z_over[1][2]()
     go_on(1)
-    z_over[2][2]()
-    go_on(2)
     for h in range(2):
         for copy in relay[h] + direct[h] + onward[h]:
             copy.wait_send()
-        z_drain(h)
+        grad_z[h][3]()
+        root_z[h][3]()
         g_over[h][0][3]()
         loop(0, ny, lambda k, h=h: g_over[h][1](k).wait_send())
-        loop(1, nz, lambda k, h=h: root_z(h, k).wait_send())
         for k in range(1, COLS):
             root_x(h, k).wait_send()
     r_drain()
@@ -541,6 +562,16 @@
     loop(1, mp, lambda k: square_send(k).wait_send())
     for over in z_over:
         over[3]()
+    loop(1, nz, lambda k: ratio_up(k).wait_recv())
+
+    def ratio_for(col):
+        return ratio_z[tab[0, z * COLS + col] // COLS]
+
+    for k in (2, 1, 3):
+        ratio_xs[k - 1] = ratio_for((x + k) % COLS)
+        ratio_on(k).start()
+    ratio_x[x] = ratio_for(x)
+    loop(1, nz, lambda k: ratio_up(k).wait_send())
     limit = tab[4, dp]
 
     def put(j):
@@ -556,11 +587,14 @@
         put(j).start()
     for k in range(1, COLS):
         fin(2, k).wait_recv()
-    home = fx[2][tab[0, dp] % COLS]
-    packed[2 * cap] = jnp.where(tab[5, dp] > 0, home, jnp.zeros_like(home))
+        ratio_on(k).wait_recv()
+    seat = tab[0, dp] % COLS
+    home = fx[2][seat].astype(f32) * ratio_x[seat][0:1, 0:1]
+    packed[2 * cap] = jnp.where(tab[5, dp] > 0, home, 0.0).astype(bf16)
     put(2).start()
-    for j in range(3):
-        for k in range(1, COLS):
+    for k in range(1, COLS):
+        ratio_on(k).wait_send()
+        for j in range(3):
             fin(j, k).wait_send()
     for j in range(3):
         put(j).wait()
@@ -658,15 +692,23 @@
         pieces(2, COLS),
         pieces(COLS),
         pieces(COLS),
-        pieces(2, nz),
         pieces(nz),
         pieces(nz),
         pieces(2, 2),
+        pieces(2, 2),
+        pieces(2),
+        pieces(2),
+        pieces(max(nz - 1, 4)),
+        pieces(max(nz - 1, 4)),
+        pieces(2, 2),
         pieces(2),
         V((128, width), f32),
-        V((rows, width), f32),
         V((8, 128), f32),
         V((mp, 8, 128), f32),
+        V((8, 128), f32),
+        V((nz, 8, 128), f32),
+        V((COLS - 1, 8, 128), f32),
+        V((COLS, 8, 128), f32),
         pieces(nz),
         pieces(nz),
         pieces(nz),
@@ -679,14 +721,14 @@
     ]
     for shape in [
         (2, COLS),
-        (2, nz - 1),
         (2, 6),
-        (2, max(nz - 1, 8)),
+        (4, max(nz - 1, 8)),
         (3, 2, 4),
         (3, ny),
         (mp - 1,),
         (3, 2, 4),
         (3, COLS - 1),
+        (2, max(nz - 1, COLS - 1)),
     ]:
         scratch += [D(shape), D(shape)]
     anywhere = pl.BlockSpec(memory_space=pltpu.HBM)

time: 72.5 us -> 70.9 us (0.978)
  Pallas kernels: 71.7 us -> 70.1 us
    pallas_call x1, Pallas kernels: 69.8 us -> 68.2 us  [shards(): pl.pallas_call(functools.partial(kernel, sizes), out_shape=jax.ShapeDtype...]
where the time goes in v4:
time: 70.9 us; the launch traced here: 70.7 us
  Pallas kernels  70.1 us (99%)
    pallas_call x1, Pallas kernels, shards(): pl.pallas_call(functools.partial(kernel, sizes), out_shape=jax.ShapeDtype...  68.2 us
    pallas_call x1, Pallas kernels, shards(): pl.pallas_call(finish, out_shape=(jax.ShapeDtypeStruct((1, rows, width),...  1.9 us

profile of v4, /device:TPU:1, one launch (start us, length us, event | category | flops | bytes accessed | tf_op | source)
XLA Modules:
  0.0 70.7 jit_solution(8411959878135271105)
XLA Ops:
  0.6 68.2 %shampoo.1.result = bf16[9,32,512]{2,1,0:T(8,128)(2,1)} custom-call(s32[1,32]{1,0:T(1,128)} %bitcast.2, s32[1,32]{1,0:T(1,128)} %bitcast.3, bf16[1024,512]{1,0:T(8,128)(2,1)} %acts.1, bf16[1024,1024]{1,0:T(8,128)(2,1)} %cot.1, bf16[4,32,512]{2,1,0:T(8,128)(2,1)} %lroot.1, bf16[4,32,512]{2,1,0:T(8,128)(2,1)} %rroot.1), custom_call_target="tpu_custom_call" | custom-call | tf_op jit(solution)/shard_map/shampoo/pallas_call | solution.py:735
  68.8 1.9 %finish.1 = (bf16[1,32,512]{2,1,0:T(8,128)(2,1)}, f32[4,32,512]{2,1,0:T(8,128)}, f32[4,32,512]{2,1,0:T(8,128)}) custom-call(bf16[9,32,512]{2,1,0:T(8,128)(2,1)} %shampoo.1.result, f32[4,32,512]{2,1,0:T(8,128)} %lstat.1, f32[4,32,512]{2,1,0:T(8,128)} %rstat.1), custom_call_target="tpu_custom_call" | custom-call | tf_op jit(solution)/shard_map/finish/pallas_call | solution.py:744

commit v5 on v4

--- a/solution.py
+++ b/solution.py
@@ -67,11 +67,16 @@
     ratio_xs,
     ratio_x,
     zb_l,
-    zb_r,
+    zb_r0,
+    zb_r1,
     zb_u,
-    fxs,
+    fxs_l,
+    fxs_r0,
+    fxs_r1,
+    fxs_u,
     fx_l,
-    fx_r,
+    fx_r0,
+    fx_r1,
     fx_u,
     packed,
     loc,
@@ -100,8 +105,9 @@
     x, z = dp % COLS, dp // COLS
     c, y = m % 2, m // 2
     half = nz // 2
-    rx, rz, zb = (rx_l, rx_r), (rz_l, rz_r), (zb_l, zb_r, zb_u)
-    fx = (fx_l, fx_r, fx_u)
+    rx, rz, zb = (rx_l, rx_r), (rz_l, rz_r), (zb_l, zb_r0, zb_r1, zb_u)
+    fx = (fx_l, fx_r0, fx_r1, fx_u)
+    fxs = (fxs_l, fxs_r0, fxs_r1, fxs_u)
     part_rows = [pl.ds(h * (rows // 2), rows // 2) for h in range(2)]
 
     def at_x(k):
@@ -345,21 +351,17 @@
         got = got.astype(bf16).reshape(part.shape[0], rows, wide)
         part[:, n // per, :, pl.ds(pl.multiple_of((n % per) * wide, wide), wide)] = got
 
-    def arrange(h):
+    def arrange(h, *cols):
         at = part_rows[h]
 
-        def one(s):
-            b = tab[2, s]
-            q[s % COLS, s // COLS, at, :] = part[b // ncol, b % ncol, at, :]
-
         def row(k):
-            for col in range(COLS):
-                one(k * COLS + col)
+            for col in cols:
+                b = tab[2, k * COLS + col]
+                q[col, k, at, :] = part[b // ncol, b % ncol, at, :]
 
         loop(0, nz, row)
 
     loop(0, c_v.shape[1] // wide, multiply)
-    arrange(0)
     lo, hi = pl.ds(0, half), pl.ds(half, half)
     far, right, left = (x + 2) % COLS, (x + 1) % COLS, (x + 3) % COLS
 
@@ -389,11 +391,16 @@
         onward.append(
             [x_copy(h, 4, fwd.at[0], xa.at[2], 1), x_copy(h, 5, fwd.at[1], xa.at[3], 3)]
         )
-    for copy in relay[0] + direct[0]:
-        copy.start()
-    arrange(1)
-    for copy in relay[1]:
-        copy.start()
+    for h in range(2):
+        arrange(h, far)
+        for copy in relay[h]:
+            copy.start()
+        arrange(h, right, left)
+        if h == 0:
+            for copy in direct[0]:
+                copy.start()
+    arrange(0, x)
+    arrange(1, x)
 
     def send_on(h):
         at = part_rows[h]
@@ -481,7 +488,7 @@
     applied = jnp.dot(left_root, g, preferred_element_type=f32).astype(bf16)
     cond = jnp.dot(applied, rful[...].reshape(order, width), preferred_element_type=f32)
     zb_u[z] = cond.astype(bf16)
-    z_over[2][0](0)
+    z_over[3][0](0)
     partial_sum = jnp.broadcast_to(jnp.sum(cond * cond, keepdims=True), ssq_s.shape)
     ssq_s[...] = partial_sum
     ssq[m] = partial_sum
@@ -499,11 +506,13 @@
     piece = pl.multiple_of((m * rows // 128) * 128, 128)
     columns = gful[:, :, pl.ds(piece, 128)].reshape(order, 128)
     slab[...] = lax.dot_general(columns, g, (((0,), (0,)), ((), ())), preferred_element_type=f32)
-    zb_r[z] = slab[pl.ds((m * rows) % 128, rows), :].astype(bf16)
-    z_over[1][0](0)
+    for h, place in enumerate((zb_r0, zb_r1)):
+        at = pl.ds((m * rows) % 128 + h * (rows // 2), rows // 2)
+        place[z] = slab[at, :].astype(bf16)
+        z_over[1 + h][0](0)
     wide_g = g.astype(f32)
     grad_square = jnp.sum(wide_g * wide_g, keepdims=True)
-    z_over[2][1]()
+    z_over[3][1]()
     z_over[0][1]()
     loop(1, mp, lambda k: square_send(k).wait_recv())
     cond_square = jnp.sum(ssq[...], axis=0)[0:1, 0:1]
@@ -522,6 +531,7 @@
 
     loop(1, nz, lambda k: ratio_up(k).start())
     z_over[1][1]()
+    z_over[2][1]()
 
     def seat_row(col):
         begin = tab[1, z * COLS + col]
@@ -530,24 +540,26 @@
 
     def fin(j, k):
         return send(
-            fxs.at[j, k - 1], fx[j].at[x], s_fx.at[j, k - 1], r_fx.at[j, k - 1], at_x(k)
+            fxs[j].at[k - 1], fx[j].at[x], s_fx.at[j, k - 1], r_fx.at[j, k - 1], at_x(k)
         )
 
     def go_on(j):
         def pick(col):
-            return zb[j][seat_row(col) if j < 2 else tab[0, z * COLS + col] // COLS]
+            return zb[j][seat_row(col) if j < 3 else tab[0, z * COLS + col] // COLS]
 
         for k in (2, 1, 3):
-            fxs[j, k - 1] = pick((x + k) % COLS)
+            fxs[j][k - 1] = pick((x + k) % COLS)
             fin(j, k).start()
         fx[j][x] = pick(x)
 
-    z_over[2][2]()
-    go_on(2)
+    z_over[3][2]()
+    go_on(3)
     z_over[0][2]()
     go_on(0)
     z_over[1][2]()
     go_on(1)
+    z_over[2][2]()
+    go_on(2)
     for h in range(2):
         for copy in relay[h] + direct[h] + onward[h]:
             copy.wait_send()
@@ -578,23 +590,25 @@
         at = pl.ds(j * cap, cap if j < 2 else 1)
         return pltpu.make_async_copy(packed.at[at], result.at[at], loc.at[7 + j])
 
-    for j in range(2):
+    for j in range(3):
         for k in range(1, COLS):
             fin(j, k).wait_recv()
+        at = every if j == 0 else part_rows[j - 1]
         for r in range(cap):
             add = fx[j][(start_me + r) % COLS]
-            packed[j * cap + r] = jnp.where(limit > r, add, jnp.zeros_like(add))
-        put(j).start()
+            packed[min(j, 1) * cap + r, at, :] = jnp.where(limit > r, add, jnp.zeros_like(add))
+        if j != 1:
+            put(min(j, 1)).start()
     for k in range(1, COLS):
-        fin(2, k).wait_recv()
+        fin(3, k).wait_recv()
         ratio_on(k).wait_recv()
     seat = tab[0, dp] % COLS
-    home = fx[2][seat].astype(f32) * ratio_x[seat][0:1, 0:1]
+    home = fx[3][seat].astype(f32) * ratio_x[seat][0:1, 0:1]
     packed[2 * cap] = jnp.where(tab[5, dp] > 0, home, 0.0).astype(bf16)
     put(2).start()
     for k in range(1, COLS):
         ratio_on(k).wait_send()
-        for j in range(3):
+        for j in range(4):
             fin(j, k).wait_send()
     for j in range(3):
         put(j).wait()
@@ -710,11 +724,16 @@
         V((COLS - 1, 8, 128), f32),
         V((COLS, 8, 128), f32),
         pieces(nz),
+        V((nz, rows // 2, width), bf16),
+        V((nz, rows // 2, width), bf16),
         pieces(nz),
-        pieces(nz),
-        pieces(3, COLS - 1),
+        pieces(COLS - 1),
+        V((COLS - 1, rows // 2, width), bf16),
+        V((COLS - 1, rows // 2, width), bf16),
+        pieces(COLS - 1),
         pieces(COLS),
-        pieces(COLS),
+        V((COLS, rows // 2, width), bf16),
+        V((COLS, rows // 2, width), bf16),
         pieces(COLS),
         pieces(2 * cap + 1),
         D((10,)),
@@ -726,8 +745,8 @@
         (3, 2, 4),
         (3, ny),
         (mp - 1,),
-        (3, 2, 4),
-        (3, COLS - 1),
+        (4, 2, 4),
+        (4, COLS - 1),
         (2, max(nz - 1, COLS - 1)),
     ]:
         scratch += [D(shape), D(shape)]

time: 70.9 us -> 70.6 us (level)
  no operation moved by 1% of the time
where the time goes in v5:
time: 70.6 us; the launch traced here: 70.5 us
  Pallas kernels  69.8 us (99%)
    pallas_call x1, Pallas kernels, shards(): pl.pallas_call(functools.partial(kernel, sizes), out_shape=jax.ShapeDtype...  67.9 us
    pallas_call x1, Pallas kernels, shards(): pl.pallas_call(finish, out_shape=(jax.ShapeDtypeStruct((1, rows, width),...  1.9 us

profile of v5, /device:TPU:1, one launch (start us, length us, event | category | flops | bytes accessed | tf_op | source)
XLA Modules:
  0.0 70.5 jit_solution(9457713489014938165)
XLA Ops:
  0.6 67.9 %shampoo.1.result = bf16[9,32,512]{2,1,0:T(8,128)(2,1)} custom-call(s32[1,32]{1,0:T(1,128)} %bitcast.2, s32[1,32]{1,0:T(1,128)} %bitcast.3, bf16[1024,512]{1,0:T(8,128)(2,1)} %acts.1, bf16[1024,1024]{1,0:T(8,128)(2,1)} %cot.1, bf16[4,32,512]{2,1,0:T(8,128)(2,1)} %lroot.1, bf16[4,32,512]{2,1,0:T(8,128)(2,1)} %rroot.1), custom_call_target="tpu_custom_call" | custom-call | tf_op jit(solution)/shard_map/shampoo/pallas_call | solution.py:754
  68.6 1.9 %finish.1 = (bf16[1,32,512]{2,1,0:T(8,128)(2,1)}, f32[4,32,512]{2,1,0:T(8,128)}, f32[4,32,512]{2,1,0:T(8,128)}) custom-call(bf16[9,32,512]{2,1,0:T(8,128)(2,1)} %shampoo.1.result, f32[4,32,512]{2,1,0:T(8,128)} %lstat.1, f32[4,32,512]{2,1,0:T(8,128)} %rstat.1), custom_call_target="tpu_custom_call" | custom-call | tf_op jit(solution)/shard_map/finish/pallas_call | solution.py:763
